TPU v7x, 32 devices: a whole 2x2x4 slice. The times are simulated.
32 devices in a mesh: gx: 2 (over y), gy: 4 (over x, core), gz: 4 (over z).
Axes of the slice: x: 2, y: 2, z: 4, core: 2. Of those that a mesh axis runs over, the one named last changes fastest.
Arguments:
- coordinates: float32 [2, 4, 4, 3, 16, 128], P('gx', 'gy', 'gz'), may hold values from -8 to 88
- neighbours: int32 [2, 4, 4, 16, 128], P('gx', 'gy', 'gz'), may hold values from 0 to 991, as said below
- pair_index: int32 [2, 4, 4, 4, 15360], P('gx', 'gy', 'gz'), may hold values from 0 to 127, as said below
- pair_live: int32 [2, 4, 4, 15360], P('gx', 'gy', 'gz'), may hold values 0 or 1
- basis: bfloat16 [2, 4, 4, 128, 1536], P('gx', 'gy', 'gz'), may hold values from -50 to 50
Outputs:
- next_basis: float32 [2, 4, 4, 128, 1536], P('gx', 'gy', 'gz')
- ritz_matrix: float32 [256, 256], replicated
Inputs may be any that keep to these rules, and one draw needn't show every extreme that they name: neighbours[x, y, z, 0, f] = 864 + f. Any other entry c < 864 names frame c % 32 of the domain offset by (c // 32 // 9 - 1, c // 32 // 3 % 3 - 1, c // 32 % 3 - 1), which lies in the grid and is not the domain itself; an entry c >= 864 names the domain's own frame c - 864, never the row's frame f. `pair_index`: row 0 holds a frame f < 128, row 1 a slot 1 to 15, rows 2 and 3 atoms below 16.
All inputs are finite; a program needn't handle non-finite values. No bound on the sum of `pair_live` on one device may be relied on, other than what follows from the above.
Results may differ from a plain program's by a relative error of at most 0.0003.
Values may be sent and summed in bfloat16 or wider, within the bound.
No kernel may reach another device: no remote copies, remote signals or barrier semaphores. Data moves between devices by JAX's collectives and lax.ppermute only.
A program may use at most 128 MiB of HBM per device.

v0:
```python
import jax
import jax.numpy as jnp
from jax import lax
from jax.sharding import PartitionSpec as P

stiffness = 0.01


def padded(cells, sides, width):
    for axis, dim in sides:
        count = lax.axis_size(axis)
        ends = count - 1
        head = lax.slice_in_dim(cells, 0, width, axis=dim)
        tail = lax.slice_in_dim(cells, cells.shape[dim] - width, cells.shape[dim], axis=dim)
        cells = jnp.concatenate(
            [
                lax.ppermute(tail, axis, [(i, (i + 1) % count) for i in range(ends)]),
                cells,
                lax.ppermute(head, axis, [((i + 1) % count, i) for i in range(ends)]),
            ],
            axis=dim,
        )
    return cells


def cross_product(left, right):
    return jnp.stack(
        [
            left[1] * right[2] - left[2] * right[1],
            left[2] * right[0] - left[0] * right[2],
            left[0] * right[1] - left[1] * right[0],
        ]
    )


def assemble(visible, neighbours, pair_index, pair_live):
    columns = visible.shape[2]
    frames = neighbours.shape[1]
    slots = neighbours.shape[0]
    centres = jnp.mean(visible, axis=1)
    own_frame = pair_index[0]
    slot_of = pair_index[1]
    atom_a = pair_index[2]
    atom_b = pair_index[3]
    self_column = own_frame + (columns - frames)
    partner = jnp.take(neighbours.reshape(-1), slot_of * frames + own_frame, axis=0)
    flat_coords = visible.reshape(3, -1)
    pos_a = jnp.take(flat_coords, atom_a * columns + self_column, axis=1)
    pos_b = jnp.take(flat_coords, atom_b * columns + partner, axis=1)
    arm_a = pos_a - jnp.take(centres, self_column, axis=1)
    arm_b = pos_b - jnp.take(centres, partner, axis=1)
    spring = pos_a - pos_b
    length_sq = jnp.maximum(jnp.sum(spring * spring, axis=0), 1.0)
    weight = stiffness * pair_live.astype(jnp.float32) / length_sq
    left_vec = jnp.concatenate([spring, cross_product(arm_a, spring)], axis=0)
    right_vec = jnp.concatenate([spring, cross_product(arm_b, spring)], axis=0)
    off_terms = -(weight * left_vec)[:, None, :] * right_vec[None, :, :]
    self_terms = (weight * left_vec)[:, None, :] * left_vec[None, :, :]
    values = jnp.concatenate([off_terms.reshape(36, -1).T, self_terms.reshape(36, -1).T], axis=0)
    row_keys = jnp.concatenate([slot_of * frames + own_frame, own_frame], axis=0)
    blocks = jnp.zeros((slots * frames, 36), jnp.float32).at[row_keys].add(values)
    return blocks.reshape(slots, frames, 36)


def apply_blocks(blocks, neighbours, vector_table):
    frames = neighbours.shape[1]
    vector_count = vector_table.shape[1] // 6

    def add_slot(slot_index, totals):
        gathered = jnp.take(vector_table, neighbours[slot_index], axis=0)
        coeffs = blocks[slot_index]
        pieces = [
            gathered[:, inner_dof * vector_count : (inner_dof + 1) * vector_count]
            for inner_dof in range(6)
        ]
        updated = []
        for outer_dof in range(6):
            total = totals[outer_dof]
            for inner_dof in range(6):
                column = coeffs[:, 6 * outer_dof + inner_dof : 6 * outer_dof + inner_dof + 1]
                total = total + column * pieces[inner_dof].astype(jnp.float32)
            updated.append(total)
        return tuple(updated)

    start = tuple((jnp.zeros((frames, vector_count), jnp.float32) for outer_dof in range(6)))
    totals = lax.fori_loop(0, neighbours.shape[0], add_slot, start)
    return jnp.concatenate(totals, axis=1)


def gram_matrix(left, right):
    return lax.dot_general(
        left, right, (((0,), (0,)), ((), ())), preferred_element_type=jnp.float32
    )


def rayleigh_ritz(basis_gram, cross_gram, image_gram, image_rows, total_rows):
    factor = jnp.linalg.cholesky(basis_gram / total_rows)
    sym_cross = (cross_gram + cross_gram.T) / (2.0 * total_rows)
    half_solved = lax.linalg.triangular_solve(factor, sym_cross, left_side=True, lower=True)
    ritz_matrix = lax.linalg.triangular_solve(factor, half_solved.T, left_side=True, lower=True)
    image_factor = jnp.linalg.cholesky(image_gram / total_rows)
    next_rows = lax.linalg.triangular_solve(
        image_factor, image_rows, left_side=False, lower=True, transpose_a=True
    )
    return (ritz_matrix, next_rows)


def per_device(coordinates, neighbours, pair_index, pair_live, basis):
    frames = basis.shape[3]
    vector_count = basis.shape[4] // 6
    rim_frames = frames // 4
    atoms_per = coordinates.shape[4]
    total_rows = 6 * frames * lax.axis_size("gx") * lax.axis_size("gy") * lax.axis_size("gz")
    own_basis = basis[0, 0, 0]
    own_lists = neighbours[0, 0, 0]
    flat_basis = own_basis.reshape(frames * 6, vector_count)
    basis_local = gram_matrix(flat_basis, flat_basis)
    near_coords = padded(
        coordinates[:, :, :, :, :, :rim_frames], (("gx", 0), ("gy", 1), ("gz", 2)), 1
    )
    rim_rows = basis[:, :, :, :rim_frames, :]
    near_basis = padded(rim_rows, (("gx", 0), ("gy", 1), ("gz", 2)), 1)
    ghost_coords = (
        near_coords.reshape(27, 3, atoms_per, rim_frames)
        .transpose(1, 2, 0, 3)
        .reshape(3, atoms_per, 27 * rim_frames)
    )
    visible = jnp.concatenate([ghost_coords, coordinates[0, 0, 0]], axis=2)
    blocks = assemble(visible, own_lists, pair_index[0, 0, 0], pair_live[0, 0, 0])
    vector_table = jnp.concatenate(
        [near_basis.reshape(27 * rim_frames, 6 * vector_count), own_basis], axis=0
    )
    image_rows = apply_blocks(blocks, own_lists, vector_table)
    rounded = image_rows.astype(jnp.bfloat16).reshape(frames * 6, vector_count)
    cross_local = gram_matrix(flat_basis, rounded)
    image_local = gram_matrix(rounded, rounded)
    basis_gram, cross_gram, image_gram = lax.psum(
        (basis_local, cross_local, image_local), ("gx", "gy", "gz")
    )
    ritz_matrix, next_rows = rayleigh_ritz(
        basis_gram, cross_gram, image_gram, image_rows.reshape(frames * 6, vector_count), total_rows
    )
    next_basis = next_rows.reshape(1, 1, 1, frames, 6 * vector_count)
    return (next_basis, ritz_matrix)


def solution(mesh):
    placed = (
        P("gx", "gy", "gz", None, None, None),
        P("gx", "gy", "gz", None, None),
        P("gx", "gy", "gz", None, None),
        P("gx", "gy", "gz", None),
        P("gx", "gy", "gz", None, None),
    )
    return jax.shard_map(
        per_device,
        mesh=mesh,
        in_specs=placed,
        out_specs=(P("gx", "gy", "gz", None, None), P()),
        check_vma=False,
    )
```

profile of v0, /device:TPU:0, one launch (start us, length us, event | category | flops | bytes accessed | tf_op | source)
XLA Modules:
  0.0 1079.3 jit_solution(7202841269503614940)
XLA Ops:
  7.2 4.9 collective-permute-start
  14.3 4.5 collective-permute-start.6
  24.0 84.9 %gather_fusion.1 = s32[15360]{0:T(1024)S(1)} fusion(s32[2048]{0:T(1024)S(1)} %bitcast.221, s32[15360]{0:T(1024)S(1)} %broadcast_clamp_fusion), kind=kCustom, calls=%fused_computation.5 | custom fusion | bytes 184320 | tf_op jit(solution)/shard_map/jit(_take)/gather | solution.py:46
  116.1 3.5 collective-permute-start.4
  123.3 4.7 collective-permute-done.5
  128.7 4.6 copy.145
  133.3 54.4 %gather_fusion.3 = f32[15360,3]{1,0:T(8,128)} fusion(f32[3,15872]{0,1:T(8,128)} %bitcast.223, s32[15360]{0:T(1024)S(1)} %get-tuple-element.414), kind=kCustom, calls=%fused_computation.3.clone | custom fusion | bytes 430080 | tf_op jit(solution)/shard_map/jit(_take)/gather | solution.py:49
  187.7 5.0 copy.147
  193.0 51.1 %gather_fusion.5 = f32[15360,3]{1,0:T(8,128)} fusion(f32[3,992]{0,1:T(8,128)S(1)} %broadcast_multiply_fusion.2, s32[15360]{0:T(1024)S(1)} %get-tuple-element.413), kind=kCustom, calls=%fused_computation.4.clone | custom fusion | bytes 430080 | tf_op jit(solution)/shard_map/jit(_take)/gather | solution.py:51
  244.2 5.0 copy.150
  249.2 54.4 %gather_fusion.2 = f32[15360,3]{1,0:T(8,128)} fusion(f32[3,15872]{0,1:T(8,128)} %bitcast.224, s32[15360]{0:T(1024)S(1)} %get-tuple-element.418), kind=kCustom, calls=%fused_computation.clone | custom fusion | bytes 430080 | tf_op jit(solution)/shard_map/jit(_take)/gather | solution.py:48
  303.6 5.0 copy.146
  308.7 51.1 %gather_fusion.4 = f32[15360,3]{1,0:T(8,128)} fusion(f32[3,992]{0,1:T(8,128)S(1)} %broadcast_multiply_fusion.2, s32[15360]{0:T(1024)S(1)} %get-tuple-element.417), kind=kCustom, calls=%fused_computation.1.clone | custom fusion | bytes 430080 | tf_op jit(solution)/shard_map/jit(_take)/gather | solution.py:50
  359.7 5.0 copy.149
  368.2 4.2 collective-permute-start.8
  382.8 4.4 collective-permute-start.10
  387.2 14.2 %collective-permute-start.11 = (bf16[3,3,1,32,1536]{4,3,2,1,0:T(8,128)(2,1)}, bf16[3,3,1,32,1536]{4,3,2,1,0:T(8,128)(2,1)}, u32[]{:S(2)}, u32[]{:S(2)}) collective-permute-start(bf16[3,3,1,32,1536]{4,3,2,1,0:T(8,128)(2,1)} %pad_maximum_fusion.3), channel_id=1, source_target_pairs={{1,0},{2,1},{3,2},{5,4},{6,5},{7,6},{9,8},{10,9},{11,10},{13,12},{... | collective-permute-start | bytes 2654216 | tf_op jit(solution)/shard_map/ppermute | solution.py:19
  401.5 4.2 pad_maximum_fusion
  405.7 10.3 copy.151
  416.0 163.6 %scatter_custom_fusion = f32[2048,36]{1,0:T(8,128)S(1)} fusion(s32[30720]{0:T(1024)} %bitcast.248, f32[30720,36]{1,0:T(8,128)} %copy.151, f32[]{:T(128)} %constant.163.clone.1), kind=kCustom, calls=%fused_computation.145 | custom fusion | flops 1105920 | bytes 295424 | tf_op jit(solution)/shard_map/scatter-add | solution.py:61
  582.8 217.5 %while.30 = (s32[]{:T(128)}, f32[128,256]{1,0:T(8,128)}, f32[128,256]{1,0:T(8,128)}, f32[128,256]{1,0:T(8,128)}, f32[128,256]{1,0:T(8,128)}, /*index=5*/f32[128,...) while((s32[]{:T(128)}, f32[128,256]{1,0:T(8,128)}, ...), condition=%wide.region_4.7_spmd.clone, body=%wide.region_3.6_spmd.clone.sunk | while | flops 3934339 | bytes 5604240 | solution.py:86
  808.4 134.1 %all-reduce.4.cloned.1.call-done = (f32[256,256]{0,1:T(8,128)}, f32[256,256]{0,1:T(8,128)}, f32[256,256]{0,1:T(8,128)}) async-done(((f32[256,256]{0,1:T(8,128)}, f32[256,256]{0,1:T(8,128)}, f32[256,256]{0,1:T(8,128)}), (f32[256,256]{0,1:T(8,128)}, f32[256,256]{0,1:T(8,128)}, f32[256,256]{0,1:T(8,128)})) %all-reduce.4.cloned.1.call-update) | async-done | bytes 786448 | tf_op jit(solution)/shard_map/psum | solution.py:137
  944.7 11.7 %cholesky.164 = f32[128,128]{1,0:T(8,128)S(1)} custom-call(f32[128,128]{1,0:T(8,128)S(1)} %cholesky.197), custom_call_target="Cholesky" | custom-call | tf_op jit(solution)/shard_map/jit(cholesky)/cholesky | solution.py:97
  956.5 9.8 custom-call.24
  966.8 11.7 %cholesky.181 = f32[128,128]{1,0:T(8,128)S(1)} custom-call(f32[128,128]{1,0:T(8,128)S(1)} %convolution_subtract_fusion.3), custom_call_target="Cholesky" | custom-call | tf_op jit(solution)/shard_map/jit(cholesky)/cholesky | solution.py:97
  981.2 4.0 while.31
  985.2 19.9 %custom-call.26 = f32[2,128,128]{1,2,0:T(8,128)S(1)} custom-call(f32[2,128,128]{2,1,0:T(8,128)S(1)} %get-tuple-element.242), custom_call_target="InvertDiagBlocksLowerTriangular" | custom-call | tf_op jit(solution)/shard_map/triangular_solve/custom-call.4 | solution.py:100
  1008.3 11.7 %cholesky.130 = f32[128,128]{1,0:T(8,128)S(1)} custom-call(f32[128,128]{1,0:T(8,128)S(1)} %cholesky.194), custom_call_target="Cholesky" | custom-call | tf_op jit(solution)/shard_map/jit(cholesky)/cholesky | solution.py:101
  1020.1 9.8 custom-call.23
  1030.4 11.7 %cholesky.147 = f32[128,128]{1,0:T(8,128)S(1)} custom-call(f32[128,128]{1,0:T(8,128)S(1)} %convolution_subtract_fusion.4), custom_call_target="Cholesky" | custom-call | tf_op jit(solution)/shard_map/jit(cholesky)/cholesky | solution.py:101
  1044.8 4.2 while.29
  1049.0 19.7 %custom-call.14 = f32[2,128,128]{1,2,0:T(8,128)S(1)} custom-call(f32[2,128,128]{2,1,0:T(8,128)S(1)} %get-tuple-element.201), custom_call_target="InvertDiagBlocksLowerTriangular" | custom-call | tf_op jit(solution)/shard_map/triangular_solve | solution.py:102
  (366 shorter events, 281.3 us)
Async XLA Ops:
  7.2 16.8 %copy-start = (s32[1,1,1,16,128]{4,3,2,1,0:T(8,128)S(1)}, s32[1,1,1,16,128]{4,3,2,1,0:T(8,128)}, u32[]{:S(2)}) copy-start(s32[1,1,1,16,128]{4,3,2,1,0:T(8,128)} %param.15) | copy-start | bytes 24580
  7.2 935.3 %all-reduce.4.cloned.1.call-start = ((), (), s32[]{:S(2)}) async-start(), calls=%async_computation | async-start | bytes 1572864 | tf_op jit(solution)/shard_map/psum | solution.py:137
  7.2 102.6 %collective-permute-start = (f32[1,1,1,3,16,32]{5,4,3,2,1,0:T(8,128)}, f32[1,1,1,3,16,32]{5,4,3,2,1,0:T(8,128)S(1)}, u32[]{:S(2)}, u32[]{:S(2)}) collective-permute-start(f32[1,1,1,3,16,32]{5,4,3,2,1,0:T(8,128)} %bitcast.240), channel_id=1, source_target_pairs={{0,16},{1,17},{2,18},{3,19},{4,20},{5,21},{6,22},{7,23},{8,24},{9,... | collective-permute-start | bytes 18440 | tf_op jit(solution)/shard_map/ppermute | solution.py:17
  12.1 97.7 %collective-permute-start.1 = (f32[1,1,1,3,16,32]{5,4,3,2,1,0:T(8,128)}, f32[1,1,1,3,16,32]{5,4,3,2,1,0:T(8,128)S(1)}, u32[]{:S(2)}, u32[]{:S(2)}) collective-permute-start(f32[1,1,1,3,16,32]{5,4,3,2,1,0:T(8,128)} %bitcast.241), channel_id=1, source_target_pairs={{16,0},{17,1},{18,2},{19,3},{20,4},{21,5},{22,6},{23,7},{24,8},{25... | collective-permute-start | bytes 18440 | tf_op jit(solution)/shard_map/ppermute | solution.py:19
  14.3 352.2 %collective-permute-start.6 = (bf16[1,1,1,32,1536]{4,3,2,1,0:T(8,128)(2,1)S(1)}, bf16[1,1,1,32,1536]{4,3,2,1,0:T(8,128)(2,1)S(1)}, u32[]{:S(2)}, u32[]{:S(2)}) collective-permute-start(bf16[1,1,1,32,1536]{4,3,2,1,0:T(8,128)(2,1)S(1)} %slice.420), channel_id=1, source_target_pairs={{0,16},{1,17},{2,18},{3,19},{4,20},{5,21},{6,22},{7,23},{8,24},{9,... | collective-permute-start | bytes 294920 | tf_op jit(solution)/shard_map/ppermute | solution.py:17
  18.9 347.7 %collective-permute-start.7 = (bf16[1,1,1,32,1536]{4,3,2,1,0:T(8,128)(2,1)S(1)}, bf16[1,1,1,32,1536]{4,3,2,1,0:T(8,128)(2,1)}, u32[]{:S(2)}, u32[]{:S(2)}) collective-permute-start(bf16[1,1,1,32,1536]{4,3,2,1,0:T(8,128)(2,1)S(1)} %slice.420), channel_id=1, source_target_pairs={{16,0},{17,1},{18,2},{19,3},{20,4},{21,5},{22,6},{23,7},{24,8},{25... | collective-permute-start | bytes 294920 | tf_op jit(solution)/shard_map/ppermute | solution.py:19
  23.9 85.9 %copy-start.7 = (f32[1,1,1,3,16,128]{5,4,3,2,1,0:T(8,128)S(1)}, f32[1,1,1,3,16,128]{5,4,3,2,1,0:T(8,128)}, u32[]{:S(2)}) copy-start(f32[1,1,1,3,16,128]{5,4,3,2,1,0:T(8,128)} %param.14) | copy-start | bytes 73732
  23.9 88.6 %copy-start.4 = (bf16[1,1,1,128,1536]{4,3,2,1,0:T(8,128)(2,1)S(1)}, bf16[1,1,1,128,1536]{4,3,2,1,0:T(8,128)(2,1)}, u32[]{:S(2)}) copy-start(bf16[1,1,1,128,1536]{4,3,2,1,0:T(8,128)(2,1)} %param.18) | copy-start | bytes 1179652
  109.9 3.0 collective-permute-start.2
  111.2 4.9 collective-permute-start.3
  112.9 20.4 %copy-start.2 = (bf16[768,256]{1,0:T(8,128)(2,1)}, bf16[768,256]{1,0:T(8,128)(2,1)S(1)}, u32[]{:S(2)}) copy-start(bf16[768,256]{1,0:T(8,128)(2,1)S(1)} %reshape_squeeze.7) | copy-start | bytes 1179652
  116.1 7.3 collective-permute-start.4
  119.6 8.4 collective-permute-start.5
  368.2 12.5 %collective-permute-start.8 = (bf16[3,1,1,32,1536]{4,3,2,1,0:T(8,128)(2,1)}, bf16[3,1,1,32,1536]{4,3,2,1,0:T(8,128)(2,1)}, u32[]{:S(2)}, u32[]{:S(2)}) collective-permute-start(bf16[3,1,1,32,1536]{4,3,2,1,0:T(8,128)(2,1)} %pad_maximum_fusion.8), channel_id=1, source_target_pairs={{0,4},{4,8},{8,12},{1,5},{5,9},{9,13},{2,6},{6,10},{10,14},{3,7},{... | collective-permute-start | bytes 884744 | tf_op jit(solution)/shard_map/ppermute | solution.py:17
  372.4 8.3 collective-permute-start.9
  377.3 24.2 %copy-start.1 = (f32[36,15360]{1,0:T(8,128)S(1)}, f32[36,15360]{1,0:T(8,128)}, u32[]{:S(2)}) copy-start(f32[36,15360]{1,0:T(8,128)} %mul.1049) | copy-start | bytes 6635524
  382.8 197.9 %collective-permute-start.10 = (bf16[3,3,1,32,1536]{4,3,2,1,0:T(8,128)(2,1)}, bf16[3,3,1,32,1536]{4,3,2,1,0:T(8,128)(2,1)}, u32[]{:S(2)}, u32[]{:S(2)}) collective-permute-start(bf16[3,3,1,32,1536]{4,3,2,1,0:T(8,128)(2,1)} %pad_maximum_fusion.3), channel_id=1, source_target_pairs={{0,1},{1,2},{2,3},{4,5},{5,6},{6,7},{8,9},{9,10},{10,11},{12,13},{... | collective-permute-start | bytes 2654216 | tf_op jit(solution)/shard_map/ppermute | solution.py:17
  387.2 193.4 %collective-permute-start.11 = (bf16[3,3,1,32,1536]{4,3,2,1,0:T(8,128)(2,1)}, bf16[3,3,1,32,1536]{4,3,2,1,0:T(8,128)(2,1)}, u32[]{:S(2)}, u32[]{:S(2)}) collective-permute-start(bf16[3,3,1,32,1536]{4,3,2,1,0:T(8,128)(2,1)} %pad_maximum_fusion.3), channel_id=1, source_target_pairs={{1,0},{2,1},{3,2},{5,4},{6,5},{7,6},{9,8},{10,9},{11,10},{13,12},{... | collective-permute-start | bytes 2654216 | tf_op jit(solution)/shard_map/ppermute | solution.py:19
  800.2 6.0 copy-start.3
  942.5 62.6 %copy-start.6 = (f32[256,256]{0,1:T(8,128)S(1)}, f32[256,256]{0,1:T(8,128)}, u32[]{:S(2)}) copy-start(f32[256,256]{0,1:T(8,128)} %get-tuple-element.340) | copy-start | bytes 786436
  978.5 29.6 %copy-start.5 = (f32[256,256]{0,1:T(8,128)S(1)}, f32[256,256]{0,1:T(8,128)}, u32[]{:S(2)}) copy-start(f32[256,256]{0,1:T(8,128)} %get-tuple-element.339) | copy-start | bytes 786436
Sparse Core Ops, SparseCore 0:
  808.3 134.1 all-reduce.3
where the time goes:
time: 1090 us; the launch traced here: 1080 us
  other arithmetic  473 us (43%)
  local copies, waits for them, and re-layouts  393 us (36%)
  waiting for transfers between devices  143 us (13%)
  starting transfers between devices  43.6 us (4%)
  between operations  17.7 us (2%)
    scatter-add x1, other arithmetic, assemble(): jnp.zeros((slots * frames, 36), jnp.float32).at[row_keys].add(values)  164 us
    add x96, other arithmetic, add_slot(): total = total + column * pieces[inner_dof].astype(jnp.float32)  161 us
    psum x1, waiting for transfers between devices, per_device(): lax.psum((basis_local, cross_local, image_local), ('gx', 'gy', 'gz'))  134 us
    gather x1, local copies, waits for them, and re-layouts, assemble(): jnp.take(neighbours.reshape(-1), slot_of * frames + own_frame, axis=0)  84.9 us
    gather x2, local copies, waits for them, and re-layouts, assemble(): pos_a = jnp.take(flat_coords, atom_a * columns + self_column, axis=1)  59.5 us
    gather x2, local copies, waits for them, and re-layouts, assemble(): pos_b = jnp.take(flat_coords, atom_b * columns + partner, axis=1)  59.4 us
    gather x2, local copies, waits for them, and re-layouts, assemble(): arm_b = pos_b - jnp.take(centres, partner, axis=1)  56.1 us
    gather x2, local copies, waits for them, and re-layouts, assemble(): arm_a = pos_a - jnp.take(centres, self_column, axis=1)  56.1 us
  transfers between devices with their start and end apart: 13, of which 4 were waited for; matrix products, arithmetic and copies ran while one was open for 48% of the time, Pallas kernels for 0%

commit v1 on v0

v1 whole, which is shorter than its diff:
```python
import functools

import jax
import jax.numpy as jnp
from jax import lax
from jax.experimental import pallas as pl
from jax.experimental.pallas import tpu as pltpu
from jax.sharding import PartitionSpec as P

stiffness = 0.01
radix = 4096.0
exact = lax.Precision.HIGHEST
f32 = jnp.float32
bf16 = jnp.bfloat16


def round_up(value, step):
    return (value + step - 1) // step * step


def count_kernel(index_ref, out_ref, *, frames, half, first, steps, chunk):
    rows, lanes = out_ref.shape[1:]
    row_ids = lax.broadcasted_iota(jnp.int32, (rows, chunk), 0).astype(jnp.int16)
    lane_ids = lax.broadcasted_iota(jnp.int32, (lanes, chunk), 0).astype(jnp.int16)
    zero = jnp.zeros((), bf16)
    out_ref[...] = jnp.zeros_like(out_ref)

    def one_chunk(i, carry):
        at = pl.ds(pl.multiple_of((first + i) * chunk, 128), chunk)
        block = index_ref[:, at]
        frame, slot, atom_a, atom_b, live = [block[k : k + 1] for k in range(5)]
        high = atom_b >= half
        row = (slot - 1) * (half * half) + jnp.where(high, atom_b - half, atom_b) * half
        high_a = atom_a >= half
        row = row + jnp.where(high_a, atom_a - half, atom_a)
        lane = jnp.where(high_a, frames, 0) + frame
        value = jnp.where(high, radix, 1.0) * live.astype(f32)
        left = jnp.where(row_ids == row.astype(jnp.int16), value.astype(bf16), zero)
        right = jnp.where(lane_ids == lane.astype(jnp.int16), jnp.ones((), bf16), zero)
        both = lax.dot_general(
            left, right, (((1,), (1,)), ((), ())), preferred_element_type=f32
        )
        upper = jnp.floor(both * (1.0 / radix))
        out_ref[0] += both - upper * radix
        out_ref[1] += upper
        return carry

    lax.fori_loop(0, steps, one_chunk, 0)


def count_pairs(pair_rows, frames, slots, atoms, first, steps, chunk):
    half = atoms // 2
    rows = (slots - 1) * half * half
    vmem = pl.BlockSpec(memory_space=pltpu.VMEM)
    return pl.pallas_call(
        functools.partial(
            count_kernel, frames=frames, half=half, first=first, steps=steps, chunk=chunk
        ),
        in_specs=[vmem],
        out_specs=vmem,
        out_shape=jax.ShapeDtypeStruct((2, rows, 2 * frames), f32),
        cost_estimate=pl.CostEstimate(
            flops=2 * rows * 2 * frames * chunk * steps,
            bytes_accessed=rows * frames * 16,
            transcendentals=0,
        ),
        name="count_pairs",
    )(pair_rows)


upper_pairs = [(i, j) for i in range(6) for j in range(i, 6)]
pair_slot = {}
for _n, (_i, _j) in enumerate(upper_pairs):
    pair_slot[(_i, _j)] = _n
    pair_slot[(_j, _i)] = _n


def split3(x):
    hi = x.astype(bf16)
    rest = x - hi.astype(f32)
    mid = rest.astype(bf16)
    low = (rest - mid.astype(f32)).astype(bf16)
    return hi, mid, low


def block_kernel(*refs, pieces, base):
    count_refs = refs[:2]
    piece_refs = refs[2 : 2 + pieces]
    own_ref, index_ref, out_ref, near_scr, sum_scr, arm_scr, blk_scr = refs[2 + pieces :]
    atoms, frames = own_ref.shape[1:]
    slots = index_ref.shape[0]
    half = atoms // 2
    width = 3 * atoms
    near_scr[...] = jnp.zeros_like(near_scr)
    start = 0
    for piece in piece_refs:
        for k in range(piece.shape[0]):
            near_scr[start : start + piece.shape[1], 0:width] = piece[k]
            start += piece.shape[1]
    near = near_scr[...].T[0:width]
    own = own_ref[...].reshape(width, frames)
    parts = [jnp.concatenate([n, o], axis=1) for n, o in zip(split3(near), split3(own))]
    left = jnp.concatenate(parts, axis=0)
    rows = base + frames
    row_ids = lax.broadcasted_iota(jnp.int32, (rows, frames), 0)
    pos = [own_ref[c] for c in range(3)]
    centre = [jnp.mean(p, axis=0, keepdims=True) for p in pos]
    pos_t = [[p[h * half : (h + 1) * half] for h in range(2)] for p in pos]
    rho_t = [[p - c for p in pt] for pt, c in zip(pos_t, centre)]
    sum_scr[...] = jnp.zeros_like(sum_scr)
    arm_scr[...] = jnp.zeros_like(arm_scr)

    def one_slot(s, carry):
        pick = index_ref[pl.ds(s, 1), :]
        hot = jnp.where(row_ids == pick, 1.0, 0.0).astype(bf16)
        got = jnp.dot(left, hot, preferred_element_type=f32)
        far = got[0:width] + got[width : 2 * width] + got[2 * width : 3 * width]
        far = [far[c * atoms : (c + 1) * atoms] for c in range(3)]
        for c in range(3):
            arm_scr[c, pl.ds(s, 1), :] = jnp.mean(far[c], axis=0, keepdims=True) - centre[c]
        moments = [[None] * 6 for _ in range(2)]
        for b in range(atoms):
            at = pl.multiple_of((s - 1) * (half * half) + (b % half) * half, half)
            q = [jnp.broadcast_to(far[c][b : b + 1, :], (half, frames)) for c in range(3)]
            for h in range(2):
                lanes = slice(h * frames, (h + 1) * frames)
                n = count_refs[0][b // half, pl.ds(at, half), lanes]
                n = n + count_refs[1][b // half, pl.ds(at, half), lanes]
                d = [pos_t[c][h] - q[c] for c in range(3)]
                w = n / jnp.maximum(d[0] * d[0] + d[1] * d[1] + d[2] * d[2], 1.0)
                wd = [w * d[c] for c in range(3)]
                terms = [wd[0] * d[0], wd[0] * d[1], wd[0] * d[2], wd[1] * d[1], wd[1] * d[2], wd[2] * d[2]]
                m = moments[h]
                moments[h] = terms if m[0] is None else [x + y for x, y in zip(m, terms)]
        total = [None] * 21
        for h in range(2):
            m = moments[h]
            r = [rho_t[c][h] for c in range(3)]
            dd = [[m[0], m[1], m[2]], [m[1], m[3], m[4]], [m[2], m[4], m[5]]]
            dt = [
                [
                    r[1] * dd[i][2] - r[2] * dd[i][1],
                    r[2] * dd[i][0] - r[0] * dd[i][2],
                    r[0] * dd[i][1] - r[1] * dd[i][0],
                ]
                for i in range(3)
            ]
            tt = {}
            for j in range(3):
                col = [dt[0][j], dt[1][j], dt[2][j]]
                tt[(0, j)] = r[1] * col[2] - r[2] * col[1]
                tt[(1, j)] = r[2] * col[0] - r[0] * col[2]
                tt[(2, j)] = r[0] * col[1] - r[1] * col[0]
            for n, (i, j) in enumerate(upper_pairs):
                if j < 3:
                    x = dd[i][j]
                elif i < 3:
                    x = dt[i][j - 3]
                else:
                    x = tt[(i - 3, j - 3)]
                total[n] = x if total[n] is None else total[n] + x
        for n in range(21):
            sum_scr[n, pl.ds(s, 1), :] = jnp.sum(total[n], axis=0, keepdims=True) * stiffness
        return carry

    lax.fori_loop(1, slots, one_slot, 0)
    first = lax.broadcasted_iota(jnp.int32, (slots, frames), 0) == 0
    arm = [arm_scr[c] for c in range(3)]
    sums = [sum_scr[n] for n in range(21)]
    selfs = [jnp.sum(x, axis=0, keepdims=True) for x in sums]
    blk_scr[...] = jnp.zeros_like(blk_scr)
    out_ref[...] = jnp.zeros_like(out_ref)
    for j in range(6):
        for i in range(6):
            x = sums[pair_slot[(j, i)]]
            if i >= 3:
                p, q = (i - 2) % 3, (i - 1) % 3
                x = x - (arm[p] * sums[pair_slot[(j, q)]] - arm[q] * sums[pair_slot[(j, p)]])
            x = jnp.where(first, selfs[pair_slot[(j, i)]], -x)
            for h in range(2):
                blk_scr[j, pl.ds(2 * i + h, slots, stride=16), :] = x
        turned = blk_scr[j, 0 : slots * 16, :].T
        for h in range(turned.shape[1] // 128):
            out_ref[h, pl.ds(j, frames, stride=8), :] = turned[:, h * 128 : (h + 1) * 128]


def make_blocks(counts, pieces, own, index, base):
    slots, frames = index.shape
    vmem = pl.BlockSpec(memory_space=pltpu.VMEM)
    return pl.pallas_call(
        functools.partial(block_kernel, pieces=len(pieces), base=base),
        in_specs=[vmem] * (4 + len(pieces)),
        out_specs=vmem,
        out_shape=jax.ShapeDtypeStruct((slots // 8, frames * 8 + 8, 128), f32),
        scratch_shapes=[
            pltpu.VMEM((base, 128), f32),
            pltpu.VMEM((21, slots, frames), f32),
            pltpu.VMEM((3, slots, frames), f32),
            pltpu.VMEM((6, slots * 16 + 16, frames), f32),
        ],
        cost_estimate=pl.CostEstimate(flops=10**9, bytes_accessed=8 * 10**6, transcendentals=0),
        name="make_blocks",
    )(*counts, *pieces, own, index)


def apply_kernel(*refs, pieces, base):
    index_ref, coeff_ref = refs[:2]
    piece_refs = refs[2 : 2 + pieces]
    own_ref, image_ref, gram_ref, tab_scr, own_scr = refs[2 + pieces :]
    frames = own_ref.shape[0]
    slots = index_ref.shape[0]
    vectors = own_ref.shape[1] // 6
    tiles = own_ref.shape[1] // 128
    rim = piece_refs[0].shape[1]
    start = 0
    for piece in piece_refs:

        def fill(k, carry, piece=piece, start=start):
            at = (start + k) * (rim * 16)
            for t in range(tiles):
                part = piece[k, :, t * 128 : (t + 1) * 128].astype(f32)
                tab_scr[pl.ds(at + t, rim, stride=16), :] = part
            for t in range(tiles, 16):
                tab_scr[pl.ds(at + t, rim, stride=16), :] = jnp.zeros((rim, 128), f32)
            return carry

        lax.fori_loop(0, piece.shape[0], fill, 0)
        start += piece.shape[0]
    for t in range(16):
        if t < tiles:
            part = own_ref[:, t * 128 : (t + 1) * 128].astype(f32)
        else:
            part = jnp.zeros((frames, 128), f32)
        tab_scr[pl.ds(base * 16 + t, frames, stride=16), :] = part
    for h in range(2):
        for j in range(8):
            if j < 6:
                at = j * vectors + h * 128
                part = own_ref[:, at : at + 128].astype(f32)
            else:
                part = jnp.zeros((frames, 128), f32)
            own_scr[h, pl.ds(j, frames, stride=8), :] = part
    odd = lax.broadcasted_iota(jnp.int32, (8, slots * 16), 1) % 2 == 1

    def one_frame(f, carry):
        got = []
        for s in range(slots):
            at = pl.multiple_of(index_ref[s, f] * 16, 16)
            got.append(tab_scr[pl.ds(at, 16), :].astype(bf16))
        right = jnp.concatenate(got, axis=0)
        at = pl.multiple_of(f * 8, 8)
        coeff = jnp.concatenate([coeff_ref[h, pl.ds(at, 8), :] for h in range(slots // 8)], axis=1)
        wide = jnp.concatenate([jnp.where(odd, 0.0, coeff), jnp.where(odd, coeff, 0.0)], axis=0)
        high = wide.astype(bf16)
        low = (wide - high.astype(f32)).astype(bf16)
        res = jnp.dot(jnp.concatenate([high, low], axis=0), right, preferred_element_type=f32)
        res = res[0:16] + res[16:32]
        image_ref[pl.ds(at, 8), 0:128] = res[0:8]
        image_ref[pl.ds(at, 8), 128:256] = res[8:16]
        return carry

    lax.fori_loop(0, frames, one_frame, 0, unroll=4)
    dims = (((0,), (0,)), ((), ()))
    x = jnp.concatenate([own_scr[h, 0 : frames * 8, :] for h in range(2)], axis=1).astype(bf16)
    y = image_ref[...].astype(bf16)
    basis_gram = lax.dot_general(x, x, dims, preferred_element_type=f32)
    cross = lax.dot_general(x, y, dims, preferred_element_type=f32)
    image_gram = lax.dot_general(y, y, dims, preferred_element_type=f32)
    cross = cross + cross.T
    rows = lax.broadcasted_iota(jnp.int32, cross.shape, 0)
    cols = lax.broadcasted_iota(jnp.int32, cross.shape, 1)
    last = vectors - 1
    corner = jnp.sum(jnp.where((rows == last) & (cols == last), cross, 0.0), axis=0, keepdims=True)
    diag = jnp.where((rows == cols) & (rows < last), cross, 0.0)
    diag = pltpu.roll(diag, 1, 1) + jnp.where(rows == 0, corner, 0.0)
    gram_ref[0] = jnp.where(rows >= cols, image_gram, cross)
    gram_ref[1] = jnp.where(rows >= cols, basis_gram, diag)


def apply_blocks(index, coeff, pieces, own, base):
    slots, frames = index.shape
    vectors = own.shape[1] // 6
    vmem = pl.BlockSpec(memory_space=pltpu.VMEM)
    return pl.pallas_call(
        functools.partial(apply_kernel, pieces=len(pieces), base=base),
        in_specs=[pl.BlockSpec(memory_space=pltpu.SMEM)] + [vmem] * (2 + len(pieces)),
        out_specs=(vmem, vmem),
        out_shape=(
            jax.ShapeDtypeStruct((frames * 8, vectors), f32),
            jax.ShapeDtypeStruct((2, vectors, vectors), f32),
        ),
        scratch_shapes=[
            pltpu.VMEM(((base + frames) * 16 + 16, 128), f32),
            pltpu.VMEM((2, frames * 8 + 8, 128), f32),
        ],
        cost_estimate=pl.CostEstimate(flops=10**9, bytes_accessed=8 * 10**6, transcendentals=0),
        name="apply_blocks",
    )(index, coeff, *pieces, own)


panel = 64


def factor_panel(block):
    groups = panel // 8
    sub = lax.broadcasted_iota(jnp.int32, (8, 128), 0)
    rows = [block[g * 8 : (g + 1) * 8] for g in range(groups)]
    for g in range(groups):
        wide = [
            [jnp.broadcast_to(rows[r][:, g * 8 + k : g * 8 + k + 1], (8, 128)) for k in range(8)]
            for r in range(g, groups)
        ]
        lead = wide[0]
        top = rows[g]
        inverse = []
        scale = jnp.zeros((8, 128), f32)
        for k in range(8):
            pivot = jnp.broadcast_to(lead[k][k : k + 1, :], (8, 128))
            inv = 1.0 / pivot
            inverse.append(inv)
            scale = jnp.where(sub == k, lax.rsqrt(pivot), scale)
            factor = jnp.where(sub > k, lead[k] * inv, 0.0)
            top_row = jnp.broadcast_to(top[k : k + 1, :], (8, 128))
            top = top - factor * top_row
            for m in range(k + 1, 8):
                lead[m] = lead[m] - factor * jnp.broadcast_to(lead[m][k : k + 1, :], (8, 128))
        for r in range(g + 1, groups):
            cols = wide[r - g]
            row = rows[r]
            for k in range(8):
                factor = cols[k] * inverse[k]
                row = row - factor * jnp.broadcast_to(top[k : k + 1, :], (8, 128))
                for m in range(k + 1, 8):
                    cols[m] = cols[m] - factor * jnp.broadcast_to(lead[m][k : k + 1, :], (8, 128))
            rows[r] = row
        rows[g] = top * scale
    return jnp.concatenate(rows, axis=0)


def solve_kernel(gram_ref, image_ref, next_ref, ritz_ref, mat_scr, res_scr, *, total_rows):
    size = gram_ref.shape[1]
    frames = next_ref.shape[0]
    rows = lax.broadcasted_iota(jnp.int32, (size, size), 0)
    cols = lax.broadcasted_iota(jnp.int32, (size, size), 1)
    mixed = gram_ref[0] * (1.0 / total_rows)
    other = gram_ref[1] * (1.0 / total_rows)
    turned = mixed.T
    image_gram = jnp.where(rows >= cols, mixed, turned)
    basis_gram = jnp.where(rows >= cols, other, other.T)
    last = size - 1
    diag = pltpu.roll(jnp.where(cols == rows + 1, other, 0.0), size - 1, 1)
    corner = jnp.sum(jnp.where((rows == 0) & (cols == last), other, 0.0), axis=0, keepdims=True)
    diag = diag + jnp.where(rows == last, corner, 0.0)
    cross = jnp.where(rows < cols, mixed, jnp.where(rows > cols, turned, diag)) * 0.5
    eye = jnp.where(rows == cols, 1.0, 0.0)
    mat_scr[0, :, 0:size] = image_gram
    mat_scr[1, :, 0:size] = basis_gram
    mat_scr[0, :, size:] = eye
    mat_scr[1, :, size:] = eye
    small = jnp.where(
        lax.broadcasted_iota(jnp.int32, (panel, panel), 0)
        == lax.broadcasted_iota(jnp.int32, (panel, panel), 1),
        1.0,
        0.0,
    )
    lane_ids = lax.broadcasted_iota(jnp.int32, (panel, size), 1)
    for p in range(size // panel):
        at = p * panel
        for m in range(2):
            strip = mat_scr[m, at : at + panel, :]
            block = jnp.concatenate([strip[:, at : at + panel], small], axis=1)
            inv = factor_panel(block)[:, panel:]
            done = jnp.dot(inv, strip, precision=exact, preferred_element_type=f32)
            mat_scr[m, at : at + panel, :] = done
            if at + panel < size:
                left = jnp.where(lane_ids >= at + panel, done[:, 0:size], 0.0)
                mat_scr[m] = mat_scr[m] - lax.dot_general(
                    left, done, (((0,), (0,)), ((), ())), precision=exact, preferred_element_type=f32
                )
    image_inv = mat_scr[0, :, size:]
    basis_inv = mat_scr[1, :, size:]
    turn = (((1,), (1,)), ((), ()))
    res = lax.dot_general(image_ref[...], image_inv, turn, precision=exact, preferred_element_type=f32)
    for h in range(size // 128):
        res_scr[h, 0 : frames * 8, :] = res[:, h * 128 : (h + 1) * 128]
    for j in range(6):
        for h in range(size // 128):
            at = j * size + h * 128
            next_ref[:, at : at + 128] = res_scr[h, pl.ds(j, frames, stride=8), :]
    half = jnp.dot(basis_inv, cross, precision=exact, preferred_element_type=f32)
    ritz_ref[...] = lax.dot_general(half, basis_inv, turn, precision=exact, preferred_element_type=f32)


def solve(gram, image, total_rows):
    size = image.shape[1]
    frames = image.shape[0] // 8
    vmem = pl.BlockSpec(memory_space=pltpu.VMEM)
    return pl.pallas_call(
        functools.partial(solve_kernel, total_rows=float(total_rows)),
        in_specs=[vmem, vmem],
        out_specs=(vmem, vmem),
        out_shape=(
            jax.ShapeDtypeStruct((frames, 6 * size), f32),
            jax.ShapeDtypeStruct((size, size), f32),
        ),
        scratch_shapes=[
            pltpu.VMEM((2, size, 2 * size), f32),
            pltpu.VMEM((size // 128, frames * 8 + 8, 128), f32),
        ],
        cost_estimate=pl.CostEstimate(flops=10**9, bytes_accessed=3 * 10**6, transcendentals=0),
        name="solve",
    )(gram, image)


def spread(stack, axis):
    count = lax.axis_size(axis)
    if count == 1:
        return [stack]
    up = [(i, i + 1) for i in range(count - 1)]
    down = [(i + 1, i) for i in range(count - 1)]
    if count == 2:
        return [stack, lax.ppermute(stack, axis, up + down)]
    return [stack, lax.ppermute(stack, axis, up), lax.ppermute(stack, axis, down)]


def place_of(offset, axis):
    count = lax.axis_size(axis)
    if count <= 2:
        return jnp.where(offset == 1, 0, 1), count
    return jnp.where(offset == 1, 0, jnp.where(offset == 0, 1, 2)), 3


def collect(rim):
    first = spread(rim, "gx")
    second = spread(jnp.concatenate(first, axis=0), "gz")
    return spread(jnp.concatenate(second, axis=0), "gy")


def sum_all(values, axes, halvings):
    steps = []
    for axis in axes:
        bit = 1
        while bit < lax.axis_size(axis):
            steps.append((axis, bit))
            bit *= 2
    trail = []
    for n, (axis, bit) in enumerate(steps):
        pairs = [(i, i ^ bit) for i in range(lax.axis_size(axis))]
        if n >= halvings:
            values = values + lax.ppermute(values, axis, pairs)
            continue
        high = (lax.axis_index(axis) & bit) != 0
        half = values.shape[0] // 2
        front, back = values[:half], values[half:]
        got = lax.ppermute(jnp.where(high, front, back), axis, pairs)
        values = jnp.where(high, back, front) + got
        trail.append((axis, high, pairs))
    for axis, high, pairs in reversed(trail):
        got = lax.ppermute(values, axis, pairs)
        values = jnp.where(
            high, jnp.concatenate([got, values]), jnp.concatenate([values, got])
        )
    return values


def per_device(coordinates, neighbours, pair_index, pair_live, basis):
    frames, columns = basis.shape[3:]
    rim = frames // 4
    atoms = coordinates.shape[4]
    slots = neighbours.shape[3]
    pairs = pair_index.shape[4]
    axes = ("gx", "gy", "gz")
    total_rows = 6 * frames
    for a in axes:
        total_rows *= lax.axis_size(a)
    own_coords = coordinates[0, 0, 0]
    own_basis = basis[0, 0, 0]
    lists = neighbours[0, 0, 0]

    rim_coords = own_coords.reshape(3 * atoms, frames)[:, :rim].T[None]
    near_coords = collect(rim_coords)
    near_basis = collect(own_basis[None, :rim])

    ghost = 27 * rim
    domain = lists // rim
    px, nx = place_of(domain // 9, "gx")
    py, ny = place_of(domain // 3 % 3, "gy")
    pz, nz = place_of(domain % 3, "gz")
    base = round_up(nx * ny * nz * rim, 128)
    index = jnp.where(
        lists < ghost,
        ((py * nz + pz) * nx + px) * rim + lists % rim,
        lists - ghost + base,
    )

    chunk = 1920
    steps = pairs // chunk
    cut = steps // 2
    pair_rows = jnp.concatenate(
        [pair_index[0, 0, 0], pair_live[0, 0], jnp.zeros((3, pairs), jnp.int32)], axis=0
    )
    counts = [
        count_pairs(pair_rows, frames, slots, atoms, 0, cut, chunk),
        count_pairs(pair_rows, frames, slots, atoms, cut, steps - cut, chunk),
    ]
    coeff = make_blocks(counts, near_coords, own_coords, index, base)
    image, gram = apply_blocks(index, coeff, near_basis, own_basis, base)
    size = gram.shape[1]
    gram = sum_all(gram.reshape(2 * size, size), ("gy", "gz", "gx"), 2).reshape(2, size, size)
    next_rows, ritz = solve(gram, image, total_rows)
    return next_rows[None, None, None], ritz


def solution(mesh):
    placed = (
        P("gx", "gy", "gz", None, None, None),
        P("gx", "gy", "gz", None, None),
        P("gx", "gy", "gz", None, None),
        P("gx", "gy", "gz", None),
        P("gx", "gy", "gz", None, None),
    )
    return jax.shard_map(
        per_device,
        mesh=mesh,
        in_specs=placed,
        out_specs=(P("gx", "gy", "gz", None, None), P()),
        check_vma=False,
    )
```

time: 1090 us -> 130 us (0.12)
  other arithmetic: 473 us -> 5.72 us
  local copies, waits for them, and re-layouts: 393 us -> 3.47 us
  waiting for transfers between devices: 143 us -> 30.8 us
  Pallas kernels: 0 us -> 55.7 us
  between operations: 17.7 us -> 0.84 us
    gather x25 -> x0, local copies, waits for them, and re-layouts: 342 us -> none  [the longest x1 84.9 us: assemble(): jnp.take(neighbours.reshape(-1), slot_of * frames + own_frame, axis=0)]
    scatter-add x1 -> x0, other arithmetic: 164 us -> none  [assemble(): jnp.zeros((slots * frames, 36), jnp.float32).at[row_keys].add(values)]
    add x97 -> x5, other arithmetic: 162 us -> 1.15 us  [the longest x2 1.1 us: sum_all(): values = jnp.where(high, back, front) + got]
    psum x1 -> x0, waiting for transfers between devices: 134 us -> none  [per_device(): lax.psum((basis_local, cross_local, image_local), ('gx', 'gy', 'gz'))]
    another operation x21 -> x0, other arithmetic: 110 us -> none  [the longest x7 34.6 us: rayleigh_ritz(): image_factor = jnp.linalg.cholesky(image_gram / total_rows)]
    pallas_call x0 -> x5, Pallas kernels: none -> 55.7 us  [the longest x1 18.2 us: solve(): pl.pallas_call(functools.partial(solve_kernel, total_rows=float(total_row...]
    ppermute x12 -> x17, waiting for transfers between devices: 9.3 us -> 30.8 us  [the longest x3 12.9 us: sum_all(): values = values + lax.ppermute(values, axis, pairs)]
    select_n x34 -> x5, other arithmetic: 19.7 us -> 2.58 us  [the longest x2 1.08 us: sum_all(): got = lax.ppermute(jnp.where(high, front, back), axis, pairs)]
  transfers between devices with their start and end apart: 13 -> 17, of which waited for: 4 -> 9; matrix products, arithmetic and copies ran while one was open for 48% -> 3% of each run, Pallas kernels for 0% -> 19%
where the time goes in v1:
time: 130 us; the launch traced here: 129 us
  Pallas kernels  55.7 us (43%)
  starting transfers between devices  32.7 us (25%)
  waiting for transfers between devices  30.8 us (24%)
  other arithmetic  5.72 us (4%)
  local copies, waits for them, and re-layouts  3.47 us (3%)
    pallas_call x1, Pallas kernels, solve(): pl.pallas_call(functools.partial(solve_kernel, total_rows=float(total_row...  18.2 us
    pallas_call x2, Pallas kernels, count_pairs(): pl.pallas_call(functools.partial(count_kernel, frames=frames, half=half,...  14.8 us
    ppermute x4, starting transfers between devices, spread(): lax.ppermute(stack, axis, up)  14.2 us
    pallas_call x1, Pallas kernels, apply_blocks(): pl.pallas_call(functools.partial(apply_kernel, pieces=len(pieces), base=b...  13.3 us
    ppermute x3, waiting for transfers between devices, sum_all(): values = values + lax.ppermute(values, axis, pairs)  12.9 us
    pallas_call x1, Pallas kernels, make_blocks(): pl.pallas_call(functools.partial(block_kernel, pieces=len(pieces), base=b...  9.45 us
    ppermute x2, waiting for transfers between devices, sum_all(): got = lax.ppermute(jnp.where(high, front, back), axis, pairs)  6.76 us
    ppermute x3, starting transfers between devices, sum_all(): values = values + lax.ppermute(values, axis, pairs)  6.14 us
  transfers between devices with their start and end apart: 17, of which 9 were waited for; matrix products, arithmetic and copies ran while one was open for 3% of the time, Pallas kernels for 19%

profile of v1, /device:TPU:0, one launch (start us, length us, event | category | flops | bytes accessed | tf_op | source)
XLA Modules:
  0.0 129.3 jit_solution(17353571209234511746)
XLA Ops:
  1.4 3.0 %collective-permute-start = (f32[1,32,48]{2,1,0:T(8,128)S(1)}, f32[1,32,48]{2,1,0:T(8,128)S(1)}, u32[]{:S(2)}, u32[]{:S(2)}) collective-permute-start(f32[1,32,48]{2,1,0:T(8,128)S(1)} %bitcast.43), channel_id=1, source_target_pairs={{0,16},{16,0},{1,17},{17,1},{2,18},{18,2},{3,19},{19,3},{4,20},{20... | collective-permute-start | bytes 18440 | tf_op jit(solution)/shard_map/ppermute | solution.py:422
  4.4 0.9 slice_bitcast_fusion
  5.4 1.9 %add_add_fusion.index_ref = s32[8,15360]{1,0:T(8,128)} fusion(s32[1,15360]{1,0:T(1,128)} %bitcast.48, s32[4,15360]{1,0:T(4,128)} %bitcast.42, s32[8]{0:T(128)S(1)} %pad.22.clone), kind=kLoop, calls=%fused_computation.2 | loop fusion | flops 245760 | bytes 798752 | tf_op jit(solution)/shard_map/concatenate | solution.py:499
  7.3 2.6 %collective-permute-done.5 = bf16[1,32,1536]{2,1,0:T(8,128)(2,1)S(1)} collective-permute-done((bf16[1,32,1536]{2,1,0:T(8,128)(2,1)S(1)}, bf16[1,32,1536]{2,1,0:T(8,128)(2,1)S(1)}, u32[]{:S(2)}, u32[]{:S(2)}) %collective-permute-start.5) | collective-permute-done | bytes 98336 | tf_op jit(solution)/shard_map/ppermute | solution.py:422
  10.0 3.5 %collective-permute-start.6 = (bf16[2,32,1536]{2,1,0:T(8,128)(2,1)S(1)}, bf16[2,32,1536]{2,1,0:T(8,128)(2,1)S(1)}, u32[]{:S(2)}, u32[]{:S(2)}) collective-permute-start(bf16[2,32,1536]{2,1,0:T(8,128)(2,1)S(1)} %pad_maximum_fusion.1), channel_id=1, source_target_pairs={{0,1},{1,2},{2,3},{4,5},{5,6},{6,7},{8,9},{9,10},{10,11},{12,13},{... | collective-permute-start | bytes 589832 | tf_op jit(solution)/shard_map/ppermute | solution.py:423
  13.5 1.3 collective-permute-start.7
  14.8 7.4 %count_pairs.2.refs_0_ = f32[2,960,256]{2,1,0:T(8,128)} custom-call(s32[8,15360]{1,0:T(8,128)} %add_add_fusion.index_ref), custom_call_target="tpu_custom_call" | custom-call | flops 3774873600 | bytes 1966080 | tf_op jit(solution)/shard_map/count_pairs/pallas_call | solution.py:55
  22.2 4.5 %collective-permute-start.1 = (f32[2,32,48]{2,1,0:T(8,128)S(1)}, f32[2,32,48]{2,1,0:T(8,128)S(1)}, u32[]{:S(2)}, u32[]{:S(2)}) collective-permute-start(f32[2,32,48]{2,1,0:T(8,128)S(1)} %pad_maximum_fusion.3), channel_id=1, source_target_pairs={{0,1},{1,2},{2,3},{4,5},{5,6},{6,7},{8,9},{9,10},{10,11},{12,13},{... | collective-permute-start | bytes 36872 | tf_op jit(solution)/shard_map/ppermute | solution.py:423
  26.8 1.3 collective-permute-start.2
  28.2 1.5 %collective-permute-start.8 = (bf16[6,32,1536]{2,1,0:T(8,128)(2,1)S(1)}, bf16[6,32,1536]{2,1,0:T(8,128)(2,1)S(1)}, u32[]{:S(2)}, u32[]{:S(2)}) collective-permute-start(bf16[6,32,1536]{2,1,0:T(8,128)(2,1)S(1)} %pad_maximum_fusion.refs_2_), channel_id=1, source_target_pairs={{0,4},{4,8},{8,12},{1,5},{5,9},{9,13},{2,6},{6,10},{10,14},{3,7},{... | collective-permute-start | bytes 1769480 | tf_op jit(solution)/shard_map/ppermute | solution.py:423
  29.7 1.3 collective-permute-start.9
  31.0 7.4 %count_pairs.3.refs_1_ = f32[2,960,256]{2,1,0:T(8,128)} custom-call(s32[8,15360]{1,0:T(8,128)} %add_add_fusion.index_ref), custom_call_target="tpu_custom_call" | custom-call | flops 3774873600 | bytes 1966080 | tf_op jit(solution)/shard_map/count_pairs/pallas_call | solution.py:55
  38.4 4.7 %collective-permute-start.3 = (f32[6,32,48]{2,1,0:T(8,128)S(1)}, f32[6,32,48]{2,1,0:T(8,128)S(1)}, u32[]{:S(2)}, u32[]{:S(2)}) collective-permute-start(f32[6,32,48]{2,1,0:T(8,128)S(1)} %pad_maximum_fusion.2.refs_2_), channel_id=1, source_target_pairs={{0,4},{4,8},{8,12},{1,5},{5,9},{9,13},{2,6},{6,10},{10,14},{3,7},{... | collective-permute-start | bytes 110600 | tf_op jit(solution)/shard_map/ppermute | solution.py:423
  43.1 1.3 collective-permute-start.4
  45.1 2.5 %collective-permute-done.4.refs_4_ = f32[6,32,48]{2,1,0:T(8,128)S(1)} collective-permute-done((f32[6,32,48]{2,1,0:T(8,128)S(1)}, f32[6,32,48]{2,1,0:T(8,128)S(1)}, u32[]{:S(2)}, u32[]{:S(2)}) %collective-permute-start.4) | collective-permute-done | bytes 36896 | tf_op jit(solution)/shard_map/ppermute | solution.py:423
  48.2 9.5 %make_blocks.1.refs_1_ = f32[2,1032,128]{2,1,0:T(8,128)} custom-call(f32[2,960,256]{2,1,0:T(8,128)} %count_pairs.2.refs_0_, f32[2,960,256]{2,1,0:T(8,128)} %count_pairs.3.refs_1_, f32[6,32,48]{2,1,0:T(8,128)} %copy-done.1, f32[6,32,48]{2,1,0:T(8,128)} %copy-done.2, f32[6,32,48]{2,1,0:T(8,128)} %copy-done.3, f32[3,16,128]{2,1,0:T(8,128)} %bitcast.47, ...), custom_call_target="tpu_custom_call" | custom-call | flops 1000000000 | bytes 8000000 | tf_op jit(solution)/shard_map/make_blocks/pallas_call | solution.py:190
  57.7 0.8 copy-done.5
  58.7 13.3 %apply_blocks.1 = (f32[1024,256]{1,0:T(8,128)}, f32[2,256,256]{2,1,0:T(8,128)}) custom-call(s32[16,128]{1,0:T(8,128)} %fusion.3.refs_6_.refs_0_, f32[2,1032,128]{2,1,0:T(8,128)} %make_blocks.1.refs_1_, bf16[6,32,1536]{2,1,0:T(8,128)(2,1)} %copy-done, bf16[6,32,1536]{2,1,0:T(8,128)(2,1)} %copy-done.5, bf16[6,32,1536]{2,1,0:T(8,128)(2,1)} %copy-done.6, ...), custom_call_target="tpu_custom_call" | custom-call | flops 1000000000 | bytes 8000000 | tf_op jit(solution)/shard_map/apply_blocks/pallas_call | solution.py:284
  72.0 1.1 select_bitcast_fusion
  73.0 3.3 %collective-permute-start.10 = (f32[256,256]{1,0:T(8,128)S(1)}, f32[256,256]{1,0:T(8,128)S(1)}, u32[]{:S(2)}, u32[]{:S(2)}) collective-permute-start(f32[256,256]{1,0:T(8,128)S(1)} %select_bitcast_fusion), channel_id=1, source_target_pairs={{0,4},{4,0},{8,12},{12,8},{1,5},{5,1},{9,13},{13,9},{2,6},{6,2},{1... | collective-permute-start | bytes 786440 | tf_op jit(solution)/shard_map/ppermute | solution.py:455
  76.3 1.2 collective-permute-done.10
  77.5 1.1 bitcast_add_fusion
  78.8 5.6 %collective-permute-done.11 = f32[128,256]{1,0:T(8,128)S(1)} collective-permute-done((f32[128,256]{1,0:T(8,128)S(1)}, f32[128,256]{1,0:T(8,128)S(1)}, u32[]{:S(2)}, u32[]{:S(2)}) %collective-permute-start.11) | collective-permute-done | bytes 131104 | tf_op jit(solution)/shard_map/ppermute | solution.py:455
  84.5 2.7 %collective-permute-start.12 = (f32[128,256]{1,0:T(8,128)S(1)}, f32[128,256]{1,0:T(8,128)S(1)}, u32[]{:S(2)}, u32[]{:S(2)}) collective-permute-start(f32[128,256]{1,0:T(8,128)S(1)} %select_add_fusion), channel_id=1, source_target_pairs={{0,1},{1,0},{2,3},{3,2},{4,5},{5,4},{6,7},{7,6},{8,9},{9,8},{10,11... | collective-permute-start | bytes 393224 | tf_op jit(solution)/shard_map/ppermute | solution.py:450
  87.2 3.2 %collective-permute-done.12 = f32[128,256]{1,0:T(8,128)S(1)} collective-permute-done((f32[128,256]{1,0:T(8,128)S(1)}, f32[128,256]{1,0:T(8,128)S(1)}, u32[]{:S(2)}, u32[]{:S(2)}) %collective-permute-start.12) | collective-permute-done | bytes 131104 | tf_op jit(solution)/shard_map/ppermute | solution.py:450
  90.4 2.9 %collective-permute-start.13 = (f32[128,256]{1,0:T(8,128)S(1)}, f32[128,256]{1,0:T(8,128)S(1)}, u32[]{:S(2)}, u32[]{:S(2)}) collective-permute-start(f32[128,256]{1,0:T(8,128)S(1)} %add.60), channel_id=1, source_target_pairs={{0,2},{1,3},{2,0},{3,1},{4,6},{5,7},{6,4},{7,5},{8,10},{9,11},{10,... | collective-permute-start | bytes 393224 | tf_op jit(solution)/shard_map/ppermute | solution.py:450
  93.2 5.3 %collective-permute-done.13 = f32[128,256]{1,0:T(8,128)S(1)} collective-permute-done((f32[128,256]{1,0:T(8,128)S(1)}, f32[128,256]{1,0:T(8,128)S(1)}, u32[]{:S(2)}, u32[]{:S(2)}) %collective-permute-start.13) | collective-permute-done | bytes 131104 | tf_op jit(solution)/shard_map/ppermute | solution.py:450
  99.1 4.5 %collective-permute-done.14 = f32[128,256]{1,0:T(8,128)S(1)} collective-permute-done((f32[128,256]{1,0:T(8,128)S(1)}, f32[128,256]{1,0:T(8,128)S(1)}, u32[]{:S(2)}, u32[]{:S(2)}) %collective-permute-start.14) | collective-permute-done | bytes 131104 | tf_op jit(solution)/shard_map/ppermute | solution.py:450
  104.1 4.5 %collective-permute-done.15 = f32[128,256]{1,0:T(8,128)S(1)} collective-permute-done((f32[128,256]{1,0:T(8,128)S(1)}, f32[128,256]{1,0:T(8,128)S(1)}, u32[]{:S(2)}, u32[]{:S(2)}) %collective-permute-start.15) | collective-permute-done | bytes 131104 | tf_op jit(solution)/shard_map/ppermute | solution.py:459
  108.7 1.5 %collective-permute-done.16 = f32[256,256]{1,0:T(8,128)S(1)} collective-permute-done((f32[256,256]{1,0:T(8,128)S(1)}, f32[256,256]{1,0:T(8,128)S(1)}, u32[]{:S(2)}, u32[]{:S(2)}) %collective-permute-start.16) | collective-permute-done | bytes 262176 | tf_op jit(solution)/shard_map/ppermute | solution.py:459
  110.2 0.8 maximum_select_fusion
  111.1 18.2 %solve.1 = (f32[128,1536]{1,0:T(8,128)}, f32[256,256]{1,0:T(8,128)}) custom-call(f32[2,256,256]{2,1,0:T(8,128)} %bitcast.41, f32[1024,256]{1,0:T(8,128)} %get-tuple-element.7.image_ref), custom_call_target="tpu_custom_call" | custom-call | flops 1000000000 | bytes 3000000 | tf_op jit(solution)/shard_map/solve/pallas_call | solution.py:398
  (40 shorter events, 4.1 us)
Async XLA Ops:
  1.4 20.8 %collective-permute-start = (f32[1,32,48]{2,1,0:T(8,128)S(1)}, f32[1,32,48]{2,1,0:T(8,128)S(1)}, u32[]{:S(2)}, u32[]{:S(2)}) collective-permute-start(f32[1,32,48]{2,1,0:T(8,128)S(1)} %bitcast.43), channel_id=1, source_target_pairs={{0,16},{16,0},{1,17},{17,1},{2,18},{18,2},{3,19},{19,3},{4,20},{20... | collective-permute-start | bytes 18440 | tf_op jit(solution)/shard_map/ppermute | solution.py:422
  5.3 4.6 %collective-permute-start.5 = (bf16[1,32,1536]{2,1,0:T(8,128)(2,1)S(1)}, bf16[1,32,1536]{2,1,0:T(8,128)(2,1)S(1)}, u32[]{:S(2)}, u32[]{:S(2)}) collective-permute-start(bf16[1,32,1536]{2,1,0:T(8,128)(2,1)S(1)} %slice_bitcast_fusion), channel_id=1, source_target_pairs={{0,16},{16,0},{1,17},{17,1},{2,18},{18,2},{3,19},{19,3},{4,20},{20... | collective-permute-start | bytes 294920 | tf_op jit(solution)/shard_map/ppermute | solution.py:422
  10.0 18.1 %collective-permute-start.6 = (bf16[2,32,1536]{2,1,0:T(8,128)(2,1)S(1)}, bf16[2,32,1536]{2,1,0:T(8,128)(2,1)S(1)}, u32[]{:S(2)}, u32[]{:S(2)}) collective-permute-start(bf16[2,32,1536]{2,1,0:T(8,128)(2,1)S(1)} %pad_maximum_fusion.1), channel_id=1, source_target_pairs={{0,1},{1,2},{2,3},{4,5},{5,6},{6,7},{8,9},{9,10},{10,11},{12,13},{... | collective-permute-start | bytes 589832 | tf_op jit(solution)/shard_map/ppermute | solution.py:423
  13.5 14.6 %collective-permute-start.7 = (bf16[2,32,1536]{2,1,0:T(8,128)(2,1)S(1)}, bf16[2,32,1536]{2,1,0:T(8,128)(2,1)S(1)}, u32[]{:S(2)}, u32[]{:S(2)}) collective-permute-start(bf16[2,32,1536]{2,1,0:T(8,128)(2,1)S(1)} %pad_maximum_fusion.1), channel_id=1, source_target_pairs={{1,0},{2,1},{3,2},{5,4},{6,5},{7,6},{9,8},{10,9},{11,10},{13,12},{... | collective-permute-start | bytes 589832 | tf_op jit(solution)/shard_map/ppermute | solution.py:423
  22.2 16.1 %collective-permute-start.1 = (f32[2,32,48]{2,1,0:T(8,128)S(1)}, f32[2,32,48]{2,1,0:T(8,128)S(1)}, u32[]{:S(2)}, u32[]{:S(2)}) collective-permute-start(f32[2,32,48]{2,1,0:T(8,128)S(1)} %pad_maximum_fusion.3), channel_id=1, source_target_pairs={{0,1},{1,2},{2,3},{4,5},{5,6},{6,7},{8,9},{9,10},{10,11},{12,13},{... | collective-permute-start | bytes 36872 | tf_op jit(solution)/shard_map/ppermute | solution.py:423
  26.8 11.6 %collective-permute-start.2 = (f32[2,32,48]{2,1,0:T(8,128)S(1)}, f32[2,32,48]{2,1,0:T(8,128)S(1)}, u32[]{:S(2)}, u32[]{:S(2)}) collective-permute-start(f32[2,32,48]{2,1,0:T(8,128)S(1)} %pad_maximum_fusion.3), channel_id=1, source_target_pairs={{1,0},{2,1},{3,2},{5,4},{6,5},{7,6},{9,8},{10,9},{11,10},{13,12},{... | collective-permute-start | bytes 36872 | tf_op jit(solution)/shard_map/ppermute | solution.py:423
  28.2 10.2 %copy-start = (bf16[6,32,1536]{2,1,0:T(8,128)(2,1)}, bf16[6,32,1536]{2,1,0:T(8,128)(2,1)S(1)}, u32[]{:S(2)}) copy-start(bf16[6,32,1536]{2,1,0:T(8,128)(2,1)S(1)} %pad_maximum_fusion.refs_2_) | copy-start | bytes 1769476
  28.2 16.2 %copy-start.4 = (s32[1,1,1,16,128]{4,3,2,1,0:T(8,128)S(1)}, s32[1,1,1,16,128]{4,3,2,1,0:T(8,128)}, u32[]{:S(2)}) copy-start(s32[1,1,1,16,128]{4,3,2,1,0:T(8,128)} %param.6) | copy-start | bytes 24580
  28.2 29.5 %collective-permute-start.8 = (bf16[6,32,1536]{2,1,0:T(8,128)(2,1)S(1)}, bf16[6,32,1536]{2,1,0:T(8,128)(2,1)S(1)}, u32[]{:S(2)}, u32[]{:S(2)}) collective-permute-start(bf16[6,32,1536]{2,1,0:T(8,128)(2,1)S(1)} %pad_maximum_fusion.refs_2_), channel_id=1, source_target_pairs={{0,4},{4,8},{8,12},{1,5},{5,9},{9,13},{2,6},{6,10},{10,14},{3,7},{... | collective-permute-start | bytes 1769480 | tf_op jit(solution)/shard_map/ppermute | solution.py:423
  29.7 28.0 %collective-permute-start.9 = (bf16[6,32,1536]{2,1,0:T(8,128)(2,1)S(1)}, bf16[6,32,1536]{2,1,0:T(8,128)(2,1)S(1)}, u32[]{:S(2)}, u32[]{:S(2)}) collective-permute-start(bf16[6,32,1536]{2,1,0:T(8,128)(2,1)S(1)} %pad_maximum_fusion.refs_2_), channel_id=1, source_target_pairs={{4,0},{8,4},{12,8},{5,1},{9,5},{13,9},{6,2},{10,6},{14,10},{7,3},{... | collective-permute-start | bytes 1769480 | tf_op jit(solution)/shard_map/ppermute | solution.py:423
  38.4 9.2 %copy-start.1 = (f32[6,32,48]{2,1,0:T(8,128)}, f32[6,32,48]{2,1,0:T(8,128)S(1)}, u32[]{:S(2)}) copy-start(f32[6,32,48]{2,1,0:T(8,128)S(1)} %pad_maximum_fusion.2.refs_2_) | copy-start | bytes 110596
  38.4 6.7 %collective-permute-start.3 = (f32[6,32,48]{2,1,0:T(8,128)S(1)}, f32[6,32,48]{2,1,0:T(8,128)S(1)}, u32[]{:S(2)}, u32[]{:S(2)}) collective-permute-start(f32[6,32,48]{2,1,0:T(8,128)S(1)} %pad_maximum_fusion.2.refs_2_), channel_id=1, source_target_pairs={{0,4},{4,8},{8,12},{1,5},{5,9},{9,13},{2,6},{6,10},{10,14},{3,7},{... | collective-permute-start | bytes 110600 | tf_op jit(solution)/shard_map/ppermute | solution.py:423
  43.1 4.4 %collective-permute-start.4 = (f32[6,32,48]{2,1,0:T(8,128)S(1)}, f32[6,32,48]{2,1,0:T(8,128)S(1)}, u32[]{:S(2)}, u32[]{:S(2)}) collective-permute-start(f32[6,32,48]{2,1,0:T(8,128)S(1)} %pad_maximum_fusion.2.refs_2_), channel_id=1, source_target_pairs={{4,0},{8,4},{12,8},{5,1},{9,5},{13,9},{6,2},{10,6},{14,10},{7,3},{... | collective-permute-start | bytes 110600 | tf_op jit(solution)/shard_map/ppermute | solution.py:423
  45.1 2.5 %copy-start.2 = (f32[6,32,48]{2,1,0:T(8,128)}, f32[6,32,48]{2,1,0:T(8,128)S(1)}, u32[]{:S(2)}) copy-start(f32[6,32,48]{2,1,0:T(8,128)S(1)} %collective-permute-done.3.refs_3_) | copy-start | bytes 110596
  47.6 0.7 copy-start.3
  57.7 0.8 copy-start.5
  57.7 1.0 copy-start.6
  73.0 4.5 %collective-permute-start.10 = (f32[256,256]{1,0:T(8,128)S(1)}, f32[256,256]{1,0:T(8,128)S(1)}, u32[]{:S(2)}, u32[]{:S(2)}) collective-permute-start(f32[256,256]{1,0:T(8,128)S(1)} %select_bitcast_fusion), channel_id=1, source_target_pairs={{0,4},{4,0},{8,12},{12,8},{1,5},{5,1},{9,13},{13,9},{2,6},{6,2},{1... | collective-permute-start | bytes 786440 | tf_op jit(solution)/shard_map/ppermute | solution.py:455
  78.6 5.8 %collective-permute-start.11 = (f32[128,256]{1,0:T(8,128)S(1)}, f32[128,256]{1,0:T(8,128)S(1)}, u32[]{:S(2)}, u32[]{:S(2)}) collective-permute-start(f32[128,256]{1,0:T(8,128)S(1)} %slice_select_fusion), channel_id=1, source_target_pairs={{0,8},{4,12},{8,0},{12,4},{1,9},{5,13},{9,1},{13,5},{2,10},{6,14},... | collective-permute-start | bytes 393224 | tf_op jit(solution)/shard_map/ppermute | solution.py:455
  84.5 5.9 %collective-permute-start.12 = (f32[128,256]{1,0:T(8,128)S(1)}, f32[128,256]{1,0:T(8,128)S(1)}, u32[]{:S(2)}, u32[]{:S(2)}) collective-permute-start(f32[128,256]{1,0:T(8,128)S(1)} %select_add_fusion), channel_id=1, source_target_pairs={{0,1},{1,0},{2,3},{3,2},{4,5},{5,4},{6,7},{7,6},{8,9},{9,8},{10,11... | collective-permute-start | bytes 393224 | tf_op jit(solution)/shard_map/ppermute | solution.py:450
  90.4 8.1 %collective-permute-start.13 = (f32[128,256]{1,0:T(8,128)S(1)}, f32[128,256]{1,0:T(8,128)S(1)}, u32[]{:S(2)}, u32[]{:S(2)}) collective-permute-start(f32[128,256]{1,0:T(8,128)S(1)} %add.60), channel_id=1, source_target_pairs={{0,2},{1,3},{2,0},{3,1},{4,6},{5,7},{6,4},{7,5},{8,10},{9,11},{10,... | collective-permute-start | bytes 393224 | tf_op jit(solution)/shard_map/ppermute | solution.py:450
  98.5 5.0 %collective-permute-start.14 = (f32[128,256]{1,0:T(8,128)S(1)}, f32[128,256]{1,0:T(8,128)S(1)}, u32[]{:S(2)}, u32[]{:S(2)}) collective-permute-start(f32[128,256]{1,0:T(8,128)S(1)} %add.61), channel_id=1, source_target_pairs={{0,16},{16,0},{1,17},{17,1},{2,18},{18,2},{3,19},{19,3},{4,20},{20... | collective-permute-start | bytes 393224 | tf_op jit(solution)/shard_map/ppermute | solution.py:450
  103.6 5.0 %collective-permute-start.15 = (f32[128,256]{1,0:T(8,128)S(1)}, f32[128,256]{1,0:T(8,128)S(1)}, u32[]{:S(2)}, u32[]{:S(2)}) collective-permute-start(f32[128,256]{1,0:T(8,128)S(1)} %add.62), channel_id=1, source_target_pairs={{0,8},{4,12},{8,0},{12,4},{1,9},{5,13},{9,1},{13,5},{2,10},{6,14},... | collective-permute-start | bytes 393224 | tf_op jit(solution)/shard_map/ppermute | solution.py:459
  108.6 1.6 %collective-permute-start.16 = (f32[256,256]{1,0:T(8,128)S(1)}, f32[256,256]{1,0:T(8,128)S(1)}, u32[]{:S(2)}, u32[]{:S(2)}) collective-permute-start(f32[256,256]{1,0:T(8,128)S(1)} %maximum_select_fusion.1), channel_id=1, source_target_pairs={{0,4},{4,0},{8,12},{12,8},{1,5},{5,1},{9,13},{13,9},{2,6},{6,2},{1... | collective-permute-start | bytes 786440 | tf_op jit(solution)/shard_map/ppermute | solution.py:459

commit v2 on v1

v2 whole, which is shorter than its diff:
```python
import functools

import jax
import jax.numpy as jnp
from jax import lax
from jax.experimental import pallas as pl
from jax.experimental.pallas import tpu as pltpu
from jax.sharding import PartitionSpec as P

stiffness = 0.01
radix = 4096.0
exact = lax.Precision.HIGHEST
f32 = jnp.float32
bf16 = jnp.bfloat16


def near_core(x):
    return pltpu.with_memory_space_constraint(x, pltpu.VMEM)


def round_up(value, step):
    return (value + step - 1) // step * step


def count_kernel(*refs, frames, half, first, steps, chunk):
    index_ref, *before, out_ref = refs
    rows, lanes = out_ref.shape[1:]
    row_ids = lax.broadcasted_iota(jnp.int32, (rows, chunk), 0).astype(jnp.int16)
    lane_ids = lax.broadcasted_iota(jnp.int32, (lanes, chunk), 0).astype(jnp.int16)
    zero = jnp.zeros((), bf16)
    out_ref[...] = before[0][...] if before else jnp.zeros_like(out_ref)

    def one_chunk(i, carry):
        at = pl.ds(pl.multiple_of((first + i) * chunk, 128), chunk)
        block = index_ref[:, at]
        frame, slot, atom_a, atom_b, live = [block[k : k + 1] for k in range(5)]
        high = atom_b >= half
        row = (slot - 1) * (half * half) + jnp.where(high, atom_b - half, atom_b) * half
        high_a = atom_a >= half
        row = row + jnp.where(high_a, atom_a - half, atom_a)
        lane = jnp.where(high_a, frames, 0) + frame
        value = jnp.where(high, radix, 1.0) * live.astype(f32)
        left = jnp.where(row_ids == row.astype(jnp.int16), value.astype(bf16), zero)
        right = jnp.where(lane_ids == lane.astype(jnp.int16), jnp.ones((), bf16), zero)
        both = lax.dot_general(
            left, right, (((1,), (1,)), ((), ())), preferred_element_type=f32
        )
        upper = jnp.floor(both * (1.0 / radix))
        out_ref[0] += both - upper * radix
        out_ref[1] += upper
        return carry

    lax.fori_loop(0, steps, one_chunk, 0)


def count_pairs(before, table, frames, slots, atoms, first, steps, chunk):
    half = atoms // 2
    rows = (slots - 1) * half * half
    vmem = pl.BlockSpec(memory_space=pltpu.VMEM)
    return pl.pallas_call(
        functools.partial(
            count_kernel, frames=frames, half=half, first=first, steps=steps, chunk=chunk
        ),
        in_specs=[vmem] * (1 + len(before)),
        out_specs=vmem,
        out_shape=pltpu.VMEM((2, rows, 2 * frames), f32),
        cost_estimate=pl.CostEstimate(
            flops=2 * rows * 2 * frames * chunk * steps,
            bytes_accessed=rows * frames * 16,
            transcendentals=0,
        ),
        compiler_params=pltpu.CompilerParams(vmem_limit_bytes=24 << 20),
        name="count_pairs",
    )(near_core(table), *map(near_core, before))


upper_pairs = [(i, j) for i in range(6) for j in range(i, 6)]
pair_slot = {}
for _n, (_i, _j) in enumerate(upper_pairs):
    pair_slot[(_i, _j)] = _n
    pair_slot[(_j, _i)] = _n


def split3(x):
    hi = x.astype(bf16)
    rest = x - hi.astype(f32)
    mid = rest.astype(bf16)
    low = (rest - mid.astype(f32)).astype(bf16)
    return hi, mid, low


def block_kernel(*refs, pieces, base, columns):
    count_ref = refs[0]
    piece_refs = refs[1 : 1 + pieces]
    own_ref, index_ref, out_ref, near_scr, sum_scr, arm_scr, blk_scr = refs[1 + pieces :]
    atoms, frames = own_ref.shape[1:]
    slots = index_ref.shape[0]
    half = atoms // 2
    width = 3 * atoms
    near_scr[...] = jnp.zeros_like(near_scr)
    start = 0
    for piece in piece_refs:
        for k in range(piece.shape[0]):
            near_scr[start : start + piece.shape[1], :] = piece[k, :, columns:].astype(f32)
            start += piece.shape[1]
    near = near_scr[...].T[0 : 3 * width].astype(bf16)
    near = [near[k * width : (k + 1) * width] for k in range(3)]
    own = own_ref[...].reshape(width, frames)
    parts = [jnp.concatenate([n, o], axis=1) for n, o in zip(near, split3(own))]
    left = jnp.concatenate(parts, axis=0)
    rows = base + frames
    row_ids = lax.broadcasted_iota(jnp.int32, (rows, frames), 0)
    pos = [own_ref[c] for c in range(3)]
    centre = [jnp.mean(p, axis=0, keepdims=True) for p in pos]
    pos_t = [[p[h * half : (h + 1) * half] for h in range(2)] for p in pos]
    rho_t = [[p - c for p in pt] for pt, c in zip(pos_t, centre)]
    sum_scr[...] = jnp.zeros_like(sum_scr)
    arm_scr[...] = jnp.zeros_like(arm_scr)

    def one_slot(s, carry):
        pick = index_ref[pl.ds(s, 1), :]
        hot = jnp.where(row_ids == pick, 1.0, 0.0).astype(bf16)
        got = jnp.dot(left, hot, preferred_element_type=f32)
        far = got[0:width] + got[width : 2 * width] + got[2 * width : 3 * width]
        far = [far[c * atoms : (c + 1) * atoms] for c in range(3)]
        for c in range(3):
            arm_scr[c, pl.ds(s, 1), :] = jnp.mean(far[c], axis=0, keepdims=True) - centre[c]
        moments = [[None] * 6 for _ in range(2)]
        for b in range(atoms):
            at = pl.multiple_of((s - 1) * (half * half) + (b % half) * half, half)
            q = [jnp.broadcast_to(far[c][b : b + 1, :], (half, frames)) for c in range(3)]
            for h in range(2):
                lanes = slice(h * frames, (h + 1) * frames)
                n = count_ref[b // half, pl.ds(at, half), lanes]
                d = [pos_t[c][h] - q[c] for c in range(3)]
                w = n / jnp.maximum(d[0] * d[0] + d[1] * d[1] + d[2] * d[2], 1.0)
                wd = [w * d[c] for c in range(3)]
                terms = [wd[0] * d[0], wd[0] * d[1], wd[0] * d[2], wd[1] * d[1], wd[1] * d[2], wd[2] * d[2]]
                m = moments[h]
                moments[h] = terms if m[0] is None else [x + y for x, y in zip(m, terms)]
        total = [None] * 21
        for h in range(2):
            m = moments[h]
            r = [rho_t[c][h] for c in range(3)]
            dd = [[m[0], m[1], m[2]], [m[1], m[3], m[4]], [m[2], m[4], m[5]]]
            dt = [
                [
                    r[1] * dd[i][2] - r[2] * dd[i][1],
                    r[2] * dd[i][0] - r[0] * dd[i][2],
                    r[0] * dd[i][1] - r[1] * dd[i][0],
                ]
                for i in range(3)
            ]
            tt = {}
            for j in range(3):
                col = [dt[0][j], dt[1][j], dt[2][j]]
                tt[(0, j)] = r[1] * col[2] - r[2] * col[1]
                tt[(1, j)] = r[2] * col[0] - r[0] * col[2]
                tt[(2, j)] = r[0] * col[1] - r[1] * col[0]
            for n, (i, j) in enumerate(upper_pairs):
                if j < 3:
                    x = dd[i][j]
                elif i < 3:
                    x = dt[i][j - 3]
                else:
                    x = tt[(i - 3, j - 3)]
                total[n] = x if total[n] is None else total[n] + x
        for n in range(21):
            sum_scr[n, pl.ds(s, 1), :] = jnp.sum(total[n], axis=0, keepdims=True) * stiffness
        return carry

    lax.fori_loop(1, slots, one_slot, 0)
    first = lax.broadcasted_iota(jnp.int32, (slots, frames), 0) == 0
    arm = [arm_scr[c] for c in range(3)]
    sums = [sum_scr[n] for n in range(21)]
    selfs = [jnp.sum(x, axis=0, keepdims=True) for x in sums]
    blk_scr[...] = jnp.zeros_like(blk_scr)
    out_ref[...] = jnp.zeros_like(out_ref)
    for j in range(6):
        for i in range(6):
            x = sums[pair_slot[(j, i)]]
            if i >= 3:
                p, q = (i - 2) % 3, (i - 1) % 3
                x = x - (arm[p] * sums[pair_slot[(j, q)]] - arm[q] * sums[pair_slot[(j, p)]])
            x = jnp.where(first, selfs[pair_slot[(j, i)]], -x)
            for h in range(2):
                blk_scr[j, pl.ds(2 * i + h, slots, stride=17), :] = x
        turned = jnp.concatenate([blk_scr[j, s * 17 : s * 17 + 16, :] for s in range(slots)], axis=0).T
        for h in range(turned.shape[1] // 128):
            out_ref[h, pl.ds(j, frames, stride=9), :] = turned[:, h * 128 : (h + 1) * 128]


def make_blocks(counts, pieces, own, index, base, columns):
    slots, frames = index.shape
    vmem = pl.BlockSpec(memory_space=pltpu.VMEM)
    return pl.pallas_call(
        functools.partial(block_kernel, pieces=len(pieces), base=base, columns=columns),
        in_specs=[vmem] * (3 + len(pieces)),
        out_specs=vmem,
        out_shape=pltpu.VMEM((slots // 8, frames * 9 + 16, 128), f32),
        scratch_shapes=[
            pltpu.VMEM((base, pieces[0].shape[2] - columns), f32),
            pltpu.VMEM((21, slots, frames), f32),
            pltpu.VMEM((3, slots, frames), f32),
            pltpu.VMEM((6, slots * 17 + 17, frames), f32),
        ],
        cost_estimate=pl.CostEstimate(flops=10**9, bytes_accessed=8 * 10**6, transcendentals=0),
        compiler_params=pltpu.CompilerParams(vmem_limit_bytes=20 << 20),
        name="make_blocks",
    )(near_core(counts), *map(near_core, pieces), own, index)


def apply_kernel(*refs, pieces, base):
    index_ref, high_ref, coeff_ref = refs[:3]
    piece_refs = refs[3 : 3 + pieces]
    own_ref, image_ref, keep_ref, send_ref, tab_scr, image_scr = refs[3 + pieces :]
    frames = own_ref.shape[0]
    slots = index_ref.shape[0]
    vectors = own_ref.shape[1] // 6
    tiles = own_ref.shape[1] // 128
    pitch = tiles + 1
    rim = piece_refs[0].shape[1]
    start = 0
    for piece in piece_refs:

        def fill(k, carry, piece=piece, start=start):
            at = (start + k) * (rim * pitch)
            for t in range(tiles):
                part = piece[k, :, t * 128 : (t + 1) * 128].astype(f32)
                tab_scr[pl.ds(at + t, rim, stride=pitch), :] = part
            tab_scr[pl.ds(at + tiles, rim, stride=pitch), :] = jnp.zeros((rim, 128), f32)
            return carry

        lax.fori_loop(0, piece.shape[0], fill, 0)
        start += piece.shape[0]
    for t in range(tiles):
        part = own_ref[:, t * 128 : (t + 1) * 128].astype(f32)
        tab_scr[pl.ds(base * pitch + t, frames, stride=pitch), :] = part
    tab_scr[pl.ds(base * pitch + tiles, frames, stride=pitch), :] = jnp.zeros((frames, 128), f32)
    tab_scr[(base + frames) * pitch :, :] = jnp.zeros((16, 128), f32)
    odd = lax.broadcasted_iota(jnp.int32, (8, slots * 16), 1) % 2 == 1

    def one_frame(f, carry):
        got = []
        for s in range(slots):
            got.append(tab_scr[pl.ds(index_ref[s, f] * pitch, 16), :].astype(bf16))
        right = jnp.concatenate(got, axis=0)
        at = f * 9
        coeff = jnp.concatenate([coeff_ref[h, pl.ds(at, 8), :] for h in range(slots // 8)], axis=1)
        wide = jnp.concatenate([jnp.where(odd, 0.0, coeff), jnp.where(odd, coeff, 0.0)], axis=0)
        high = wide.astype(bf16)
        low = (wide - high.astype(f32)).astype(bf16)
        res = jnp.dot(jnp.concatenate([high, low], axis=0), right, preferred_element_type=f32)
        res = res[0:16] + res[16:32]
        image_scr[0, pl.ds(at, 8), :] = res[0:8]
        image_scr[1, pl.ds(at, 8), :] = res[8:16]
        return carry

    lax.fori_loop(0, frames, one_frame, 0, unroll=4)
    dims = (((0,), (0,)), ((), ()))
    basis_gram = jnp.zeros((vectors, vectors), f32)
    cross = jnp.zeros((vectors, vectors), f32)
    image_gram = jnp.zeros((vectors, vectors), f32)
    for j in range(6):
        x = own_ref[:, j * vectors : (j + 1) * vectors]
        y = jnp.concatenate([image_scr[h, pl.ds(j, frames, stride=9), :] for h in range(2)], axis=1)
        image_ref[j * frames : (j + 1) * frames, :] = y
        y = y.astype(bf16)
        basis_gram = basis_gram + lax.dot_general(x, x, dims, preferred_element_type=f32)
        cross = cross + lax.dot_general(x, y, dims, preferred_element_type=f32)
        image_gram = image_gram + lax.dot_general(y, y, dims, preferred_element_type=f32)
    cross = cross + cross.T
    rows = lax.broadcasted_iota(jnp.int32, cross.shape, 0)
    cols = lax.broadcasted_iota(jnp.int32, cross.shape, 1)
    last = vectors - 1
    corner = jnp.sum(jnp.where((rows == last) & (cols == last), cross, 0.0), axis=0, keepdims=True)
    diag = jnp.where((rows == cols) & (rows < last), cross, 0.0)
    diag = pltpu.roll(diag, 1, 1) + jnp.where(rows == 0, corner, 0.0)
    front = jnp.where(rows >= cols, image_gram, cross)
    back = jnp.where(rows >= cols, basis_gram, diag)
    high = high_ref[0] != 0
    keep_ref[...] = jnp.where(high, back, front)
    send_ref[...] = jnp.where(high, front, back)


def apply_blocks(index, high, coeff, pieces, own, base):
    slots, frames = index.shape
    vectors = own.shape[1] // 6
    vmem = pl.BlockSpec(memory_space=pltpu.VMEM)
    return pl.pallas_call(
        functools.partial(apply_kernel, pieces=len(pieces), base=base),
        in_specs=[pl.BlockSpec(memory_space=pltpu.SMEM)] * 2 + [vmem] * (2 + len(pieces)),
        out_specs=(vmem, vmem, vmem),
        out_shape=(
            pltpu.VMEM((frames * 6, vectors), f32),
            pltpu.VMEM((vectors, vectors), f32),
            pltpu.VMEM((vectors, vectors), f32),
        ),
        scratch_shapes=[
            pltpu.VMEM(((base + frames) * (own.shape[1] // 128 + 1) + 16, 128), f32),
            pltpu.VMEM((2, frames * 9 + 16, 128), f32),
        ],
        cost_estimate=pl.CostEstimate(flops=10**9, bytes_accessed=8 * 10**6, transcendentals=0),
        compiler_params=pltpu.CompilerParams(vmem_limit_bytes=24 << 20),
        name="apply_blocks",
    )(index, high, near_core(coeff), *map(near_core, pieces), own)


panel = 64


def factor_panels(blocks):
    groups = panel // 8
    sub = lax.broadcasted_iota(jnp.int32, (8, 128), 0)
    every = range(len(blocks))
    rows = [[block[g * 8 : (g + 1) * 8] for g in range(groups)] for block in blocks]

    def spread_row(x, k):
        return jnp.broadcast_to(x[k : k + 1, :], (8, 128))

    for g in range(groups):
        wide = [
            [
                [jnp.broadcast_to(rows[b][r][:, g * 8 + k : g * 8 + k + 1], (8, 128)) for k in range(8)]
                for r in range(g, groups)
            ]
            for b in every
        ]
        top = [rows[b][g] for b in every]
        full = list(top)
        scale = [jnp.zeros((8, 128), f32) for b in every]
        square = [jnp.zeros((8, 128), f32) for b in every]
        for k in range(8):
            for b in every:
                lead = wide[b][0]
                root = lax.rsqrt(spread_row(lead[k], k))
                inv = root * root
                scale[b] = jnp.where(sub == k, root, scale[b])
                square[b] = jnp.where(sub == k, inv, square[b])
                factor = jnp.where(sub != k, lead[k] * inv, 0.0)
                below = jnp.where(sub > k, factor, 0.0)
                for m in range(k + 1, 8):
                    lead[m] = lead[m] - factor * spread_row(lead[m], k)
                top[b] = top[b] - below * spread_row(top[b], k)
                full[b] = full[b] - factor * spread_row(full[b], k)
        for b in every:
            gain = full[b] * square[b]
            gain = [spread_row(gain, k) for k in range(8)]
            for r in range(g + 1, groups):
                row = rows[b][r]
                cols = wide[b][r - g]
                for k in range(8):
                    row = row - cols[k] * gain[k]
                rows[b][r] = row
        for b in every:
            rows[b][g] = top[b] * scale[b]
    return [jnp.concatenate(rows[b], axis=0) for b in every]


def solve_kernel(high_ref, mine_ref, got_ref, image_ref, next_ref, ritz_ref, image_scr, basis_scr, *, total_rows):
    size = mine_ref.shape[1]
    frames = next_ref.shape[0]
    rows = lax.broadcasted_iota(jnp.int32, (size, size), 0)
    cols = lax.broadcasted_iota(jnp.int32, (size, size), 1)
    high = high_ref[0] != 0
    mine = mine_ref[...] * (1.0 / total_rows)
    got = got_ref[...] * (1.0 / total_rows)
    mixed = jnp.where(high, got, mine)
    other = jnp.where(high, mine, got)
    turned = mixed.T
    image_gram = jnp.where(rows >= cols, mixed, turned)
    basis_gram = jnp.where(rows >= cols, other, other.T)
    last = size - 1
    diag = pltpu.roll(jnp.where(cols == rows + 1, other, 0.0), size - 1, 1)
    corner = jnp.sum(jnp.where((rows == 0) & (cols == last), other, 0.0), axis=0, keepdims=True)
    diag = diag + jnp.where(rows == last, corner, 0.0)
    cross = jnp.where(rows < cols, mixed, jnp.where(rows > cols, turned, diag)) * 0.5
    eye = jnp.where(rows == cols, 1.0, 0.0)
    scratch = (image_scr, basis_scr)
    image_scr[:, 0:size] = image_gram
    basis_scr[:, 0:size] = basis_gram
    image_scr[:, size:] = eye
    basis_scr[:, size:] = eye
    small = jnp.where(
        lax.broadcasted_iota(jnp.int32, (panel, panel), 0)
        == lax.broadcasted_iota(jnp.int32, (panel, panel), 1),
        1.0,
        0.0,
    )
    lane_ids = lax.broadcasted_iota(jnp.int32, (panel, size), 1)

    def one_panel(p, carry):
        at = pl.multiple_of(p * panel, panel)
        strips = [ref[pl.ds(at, panel), :] for ref in scratch]
        fronts = [pltpu.roll(x[:, 0:size], size - at, 1)[:, 0:panel] for x in strips]
        solved = factor_panels([jnp.concatenate([x, small], axis=1) for x in fronts])
        done = [
            jnp.dot(inv[:, panel:], x, precision=exact, preferred_element_type=f32)
            for inv, x in zip(solved, strips)
        ]
        for ref, x in zip(scratch, done):
            left = jnp.where(lane_ids >= at + panel, x[:, 0:size], 0.0)
            ref[...] = ref[...] - lax.dot_general(
                left, x, (((0,), (0,)), ((), ())), precision=exact, preferred_element_type=f32
            )
            ref[pl.ds(at, panel), :] = x
        return carry

    lax.fori_loop(0, size // panel, one_panel, 0)
    image_inv = image_scr[:, size:]
    basis_inv = basis_scr[:, size:]
    turn = (((1,), (1,)), ((), ()))
    res = lax.dot_general(image_ref[...], image_inv, turn, precision=exact, preferred_element_type=f32)
    for j in range(6):
        next_ref[:, j * size : (j + 1) * size] = res[j * frames : (j + 1) * frames]
    half = jnp.dot(basis_inv, cross, precision=exact, preferred_element_type=f32)
    ritz_ref[...] = lax.dot_general(half, basis_inv, turn, precision=exact, preferred_element_type=f32)


def solve(high, mine, got, image, total_rows):
    size = image.shape[1]
    frames = image.shape[0] // 6
    vmem = pl.BlockSpec(memory_space=pltpu.VMEM)
    return pl.pallas_call(
        functools.partial(solve_kernel, total_rows=float(total_rows)),
        in_specs=[pl.BlockSpec(memory_space=pltpu.SMEM), vmem, vmem, vmem],
        out_specs=(vmem, vmem),
        out_shape=(
            jax.ShapeDtypeStruct((frames, 6 * size), f32),
            jax.ShapeDtypeStruct((size, size), f32),
        ),
        scratch_shapes=[
            pltpu.VMEM((size, 2 * size), f32),
            pltpu.VMEM((size, 2 * size), f32),
        ],
        cost_estimate=pl.CostEstimate(flops=10**9, bytes_accessed=3 * 10**6, transcendentals=0),
        compiler_params=pltpu.CompilerParams(vmem_limit_bytes=20 << 20),
        name="solve",
    )(high, near_core(mine), near_core(got), near_core(image))


def spread(stack, axis):
    count = lax.axis_size(axis)
    if count == 1:
        return [stack]
    up = [(i, i + 1) for i in range(count - 1)]
    down = [(i + 1, i) for i in range(count - 1)]
    if count == 2:
        return [stack, lax.ppermute(stack, axis, up + down)]
    return [stack, lax.ppermute(stack, axis, up), lax.ppermute(stack, axis, down)]


def place_of(offset, axis):
    count = lax.axis_size(axis)
    if count <= 2:
        return jnp.where(offset == 1, 0, 1), count
    return jnp.where(offset == 1, 0, jnp.where(offset == 0, 1, 2)), 3


def sum_all(values, axes, done, halvings):
    steps = []
    for axis in axes:
        bit = 1
        while bit < lax.axis_size(axis):
            if (axis, bit) != done:
                steps.append((axis, bit))
            bit *= 2
    trail = []
    for n, (axis, bit) in enumerate(steps):
        pairs = [(i, i ^ bit) for i in range(lax.axis_size(axis))]
        if n >= halvings:
            values = values + lax.ppermute(values, axis, pairs)
            continue
        high = (lax.axis_index(axis) & bit) != 0
        half = values.shape[0] // 2
        front, back = values[:half], values[half:]
        got = lax.ppermute(jnp.where(high, front, back), axis, pairs)
        values = jnp.where(high, back, front) + got
        trail.append((axis, high, pairs))
    for axis, high, pairs in reversed(trail):
        got = lax.ppermute(values, axis, pairs)
        values = jnp.where(
            high, jnp.concatenate([got, values]), jnp.concatenate([values, got])
        )
    return values


def per_device(coordinates, neighbours, pair_index, pair_live, basis):
    frames, columns = basis.shape[3:]
    rim = frames // 4
    atoms = coordinates.shape[4]
    slots = neighbours.shape[3]
    count = pair_index.shape[4]
    axes = ("gx", "gy", "gz")
    total_rows = 6 * frames
    for a in axes:
        total_rows *= lax.axis_size(a)
    own_coords = coordinates[0, 0, 0]
    own_basis = basis[0, 0, 0]
    lists = neighbours[0, 0, 0]

    spots = own_coords.reshape(3 * atoms, frames)[:, :rim].T
    high = lax.reduce_precision(spots, 8, 7)
    middle = lax.reduce_precision(spots - high, 8, 7)
    width = 9 * atoms
    row = jnp.concatenate(
        [
            own_basis[:rim],
            high.astype(bf16),
            middle.astype(bf16),
            (spots - high - middle).astype(bf16),
            jnp.zeros((rim, round_up(width, 128) - width), bf16),
        ],
        axis=1,
    )
    ghost = 27 * rim
    domain = lists // rim
    px, nx = place_of(domain // 9, "gx")
    py, ny = place_of(domain // 3 % 3, "gy")
    pz, nz = place_of(domain % 3, "gz")
    base = round_up(nx * ny * nz * rim, 128)
    index = jnp.where(
        lists < ghost,
        ((py * nz + pz) * nx + px) * rim + lists % rim,
        lists - ghost + base,
    )

    chunk = 1920
    steps = count // chunk
    cut = [0, steps // 2 - 1, steps]
    table = jnp.concatenate(
        [pair_index[0, 0, 0], pair_live[0, 0], jnp.zeros((3, count), jnp.int32)], axis=0
    )
    part = jnp.concatenate(spread(row[None], "gx"), axis=0)
    table, part = lax.optimization_barrier((table, part))
    counts = count_pairs([], table, frames, slots, atoms, cut[0], cut[1] - cut[0], chunk)
    part = jnp.concatenate(spread(part, "gz"), axis=0)
    counts, part = lax.optimization_barrier((counts, part))
    near = spread(part, "gy")
    counts = count_pairs([counts], table, frames, slots, atoms, cut[1], cut[2] - cut[1], chunk)
    coeff = make_blocks(counts, near, own_coords, index, base, columns)
    axis = "gy"
    pairs = [(i, i ^ 1) for i in range(lax.axis_size(axis))]
    side = lax.axis_index(axis) % 2
    high = side[None]
    image, keep, send = apply_blocks(index, high, coeff, near, own_basis, base)
    mine = keep + lax.ppermute(send, axis, pairs)
    mine = sum_all(mine, ("gy", "gz", "gx"), (axis, 1), 1)
    got = lax.ppermute(mine, axis, pairs)
    next_rows, ritz = solve(high, mine, got, image, total_rows)
    return next_rows[None, None, None], ritz


def solution(mesh):
    placed = (
        P("gx", "gy", "gz", None, None, None),
        P("gx", "gy", "gz", None, None),
        P("gx", "gy", "gz", None, None),
        P("gx", "gy", "gz", None),
        P("gx", "gy", "gz", None, None),
    )
    return jax.shard_map(
        per_device,
        mesh=mesh,
        in_specs=placed,
        out_specs=(P("gx", "gy", "gz", None, None), P()),
        check_vma=False,
    )
```

time: 130 us -> 102 us (0.78)
  Pallas kernels: 55.7 us -> 44 us
  starting transfers between devices: 32.7 us -> 23 us
  other arithmetic: 5.72 us -> 1.39 us
  waiting for transfers between devices: 30.8 us -> 27.8 us
    ppermute x4 -> x2, starting transfers between devices: 14.2 us -> 5.05 us  [spread(): lax.ppermute(stack, axis, up)]
    ppermute x0 -> x2, starting transfers between devices: none -> 5.32 us  [the longest x1 5.25 us: per_device(): mine = keep + lax.ppermute(send, axis, pairs)]
    pallas_call x2, Pallas kernels: 14.8 us -> 10.1 us  [count_pairs(): pl.pallas_call(functools.partial(count_kernel, frames=frames, half=half,...]
    pallas_call x1, Pallas kernels: 13.3 us -> 8.96 us  [apply_blocks(): pl.pallas_call(functools.partial(apply_kernel, pieces=len(pieces), base=b...]
    ppermute x2 -> x1, starting transfers between devices: 3.54 us -> 0.16 us  [sum_all(): got = lax.ppermute(jnp.where(high, front, back), axis, pairs)]
    pallas_call x1, Pallas kernels: 9.45 us -> 6.14 us  [make_blocks(): pl.pallas_call(functools.partial(block_kernel, pieces=len(pieces), base=b...]
    ppermute x0 -> x2, waiting for transfers between devices: none -> 2.68 us  [the longest x1 1.52 us: per_device(): got = lax.ppermute(mine, axis, pairs)]
    ppermute x4 -> x2, starting transfers between devices: 5.17 us -> 2.58 us  [spread(): lax.ppermute(stack, axis, down)]
  transfers between devices with their start and end apart: 17 -> 12, of which waited for: 9 -> 9; matrix products, arithmetic and copies ran while one was open for 3% -> 1% of each run, Pallas kernels for 19% -> 10%
where the time goes in v2:
time: 102 us
  Pallas kernels  44 us (43%)
  waiting for transfers between devices  27.8 us (27%)
  starting transfers between devices  23 us (23%)
  local copies, waits for them, and re-layouts  4.72 us (5%)
  other arithmetic  1.39 us (1%)
    pallas_call x1, Pallas kernels, solve(): pl.pallas_call(functools.partial(solve_kernel, total_rows=float(total_row...  18.7 us
    ppermute x3, waiting for transfers between devices, sum_all(): values = values + lax.ppermute(values, axis, pairs)  11.8 us
    pallas_call x2, Pallas kernels, count_pairs(): pl.pallas_call(functools.partial(count_kernel, frames=frames, half=half,...  10.1 us
    pallas_call x1, Pallas kernels, apply_blocks(): pl.pallas_call(functools.partial(apply_kernel, pieces=len(pieces), base=b...  8.96 us
    pallas_call x1, Pallas kernels, make_blocks(): pl.pallas_call(functools.partial(block_kernel, pieces=len(pieces), base=b...  6.14 us
    ppermute x3, starting transfers between devices, sum_all(): values = values + lax.ppermute(values, axis, pairs)  5.85 us
    ppermute x1, waiting for transfers between devices, sum_all(): got = lax.ppermute(jnp.where(high, front, back), axis, pairs)  5.68 us
    ppermute x1, starting transfers between devices, per_device(): mine = keep + lax.ppermute(send, axis, pairs)  5.25 us
  transfers between devices with their start and end apart: 12, of which 9 were waited for; matrix products, arithmetic and copies ran while one was open for 1% of the time, Pallas kernels for 10%

profile of v2, /device:TPU:0, one launch (start us, length us, event | category | flops | bytes accessed | tf_op | source)
XLA Modules:
  0.0 101.7 jit_solution(9994031959203262435)
XLA Ops:
  0.6 0.8 copy.9
  1.5 0.9 slice_bitcast_fusion
  2.4 0.1 concatenate.19
  2.5 3.1 %collective-permute-start = (bf16[1,32,1792]{2,1,0:T(8,128)(2,1)S(1)}, bf16[1,32,1792]{2,1,0:T(8,128)(2,1)S(1)}, u32[]{:S(2)}, u32[]{:S(2)}) collective-permute-start(bf16[1,32,1792]{2,1,0:T(8,128)(2,1)S(1)} %bitcast.45), channel_id=1, source_target_pairs={{0,16},{16,0},{1,17},{17,1},{2,18},{18,2},{3,19},{19,3},{4,20},{20... | collective-permute-start | bytes 344072 | tf_op jit(solution)/shard_map/ppermute | solution.py:449
  5.5 0.1 pad.11.clone
  5.6 1.1 %add_add_fusion.refs_0_ = s32[8,15360]{1,0:T(8,128)S(1)} fusion(s32[1,15360]{1,0:T(1,128)} %bitcast.48, s32[4,15360]{1,0:T(4,128)} %bitcast.47, s32[8]{0:T(128)S(1)} %pad.11.clone), kind=kLoop, calls=%fused_computation.1 | loop fusion | flops 245760 | bytes 798752 | tf_op jit(solution)/shard_map/concatenate | solution.py:531
  6.7 2.0 %collective-permute-done = bf16[1,32,1792]{2,1,0:T(8,128)(2,1)S(1)} collective-permute-done((bf16[1,32,1792]{2,1,0:T(8,128)(2,1)S(1)}, bf16[1,32,1792]{2,1,0:T(8,128)(2,1)S(1)}, u32[]{:S(2)}, u32[]{:S(2)}) %collective-permute-start) | collective-permute-done | bytes 114720 | tf_op jit(solution)/shard_map/ppermute | solution.py:449
  8.7 3.7 %collective-permute-start.1 = (bf16[2,32,1792]{2,1,0:T(8,128)(2,1)S(1)}, bf16[2,32,1792]{2,1,0:T(8,128)(2,1)S(1)}, u32[]{:S(2)}, u32[]{:S(2)}) collective-permute-start(bf16[2,32,1792]{2,1,0:T(8,128)(2,1)S(1)} %pad_maximum_fusion.1), channel_id=1, source_target_pairs={{0,1},{1,2},{2,3},{4,5},{5,6},{6,7},{8,9},{9,10},{10,11},{12,13},{... | collective-permute-start | bytes 688136 | tf_op jit(solution)/shard_map/ppermute | solution.py:450
  12.4 1.3 %collective-permute-start.2 = (bf16[2,32,1792]{2,1,0:T(8,128)(2,1)S(1)}, bf16[2,32,1792]{2,1,0:T(8,128)(2,1)S(1)}, u32[]{:S(2)}, u32[]{:S(2)}) collective-permute-start(bf16[2,32,1792]{2,1,0:T(8,128)(2,1)S(1)} %pad_maximum_fusion.1), channel_id=1, source_target_pairs={{1,0},{2,1},{3,2},{5,4},{6,5},{7,6},{9,8},{10,9},{11,10},{13,12},{... | collective-permute-start | bytes 688136 | tf_op jit(solution)/shard_map/ppermute | solution.py:450
  13.7 3.8 %count_pairs.2.refs_1_ = f32[2,960,256]{2,1,0:T(8,128)S(1)} custom-call(s32[8,15360]{1,0:T(8,128)S(1)} %add_add_fusion.refs_0_), custom_call_target="tpu_custom_call" | custom-call | flops 2831155200 | bytes 1966080 | tf_op jit(solution)/shard_map/count_pairs/pallas_call | solution.py:60
  17.6 1.3 %copy-done.2 = f32[2,960,256]{2,1,0:T(8,128)} copy-done((f32[2,960,256]{2,1,0:T(8,128)}, f32[2,960,256]{2,1,0:T(8,128)S(1)}, u32[]{:S(2)}) %copy-start.2) | copy-done | bytes 1966104
  18.9 1.7 %collective-permute-done.2 = bf16[2,32,1792]{2,1,0:T(8,128)(2,1)S(1)} collective-permute-done((bf16[2,32,1792]{2,1,0:T(8,128)(2,1)S(1)}, bf16[2,32,1792]{2,1,0:T(8,128)(2,1)S(1)}, u32[]{:S(2)}, u32[]{:S(2)}) %collective-permute-start.2) | collective-permute-done | bytes 229408 | tf_op jit(solution)/shard_map/ppermute | solution.py:450
  20.6 1.3 %collective-permute-start.3 = (bf16[6,32,1792]{2,1,0:T(8,128)(2,1)S(1)}, bf16[6,32,1792]{2,1,0:T(8,128)(2,1)S(1)}, u32[]{:S(2)}, u32[]{:S(2)}) collective-permute-start(bf16[6,32,1792]{2,1,0:T(8,128)(2,1)S(1)} %pad_maximum_fusion.refs_1_.refs_3_), channel_id=1, source_target_pairs={{0,4},{4,8},{8,12},{1,5},{5,9},{9,13},{2,6},{6,10},{10,14},{3,7},{... | collective-permute-start | bytes 2064392 | tf_op jit(solution)/shard_map/ppermute | solution.py:450
  21.9 1.3 %collective-permute-start.4 = (bf16[6,32,1792]{2,1,0:T(8,128)(2,1)S(1)}, bf16[6,32,1792]{2,1,0:T(8,128)(2,1)S(1)}, u32[]{:S(2)}, u32[]{:S(2)}) collective-permute-start(bf16[6,32,1792]{2,1,0:T(8,128)(2,1)S(1)} %pad_maximum_fusion.refs_1_.refs_3_), channel_id=1, source_target_pairs={{4,0},{8,4},{12,8},{5,1},{9,5},{13,9},{6,2},{10,6},{14,10},{7,3},{... | collective-permute-start | bytes 2064392 | tf_op jit(solution)/shard_map/ppermute | solution.py:450
  23.3 1.5 %copy-done.3 = f32[2,960,256]{2,1,0:T(8,128)S(1)} copy-done((f32[2,960,256]{2,1,0:T(8,128)S(1)}, f32[2,960,256]{2,1,0:T(8,128)}, u32[]{:S(2)}) %copy-start.3) | copy-done | bytes 1966104
  24.9 6.3 %count_pairs.3.refs_0_ = f32[2,960,256]{2,1,0:T(8,128)S(1)} custom-call(s32[8,15360]{1,0:T(8,128)S(1)} %add_add_fusion.refs_0_, f32[2,960,256]{2,1,0:T(8,128)S(1)} %copy-done.3), custom_call_target="tpu_custom_call" | custom-call | flops 4718592000 | bytes 1966080 | tf_op jit(solution)/shard_map/count_pairs/pallas_call | solution.py:60
  31.2 6.1 %make_blocks.1.refs_2_ = f32[2,1168,128]{2,1,0:T(8,128)S(1)} custom-call(f32[2,960,256]{2,1,0:T(8,128)S(1)} %count_pairs.3.refs_0_, bf16[6,32,1792]{2,1,0:T(8,128)(2,1)S(1)} %pad_maximum_fusion.refs_1_.refs_3_, bf16[6,32,1792]{2,1,0:T(8,128)(2,1)S(1)} %collective-permute-done.3.refs_2_.refs_4_, ...), custom_call_target="tpu_custom_call" | custom-call | flops 1000000000 | bytes 8000000 | tf_op jit(solution)/shard_map/make_blocks/pallas_call | solution.py:196
  37.4 9.0 %apply_blocks.1 = (f32[768,256]{1,0:T(8,128)S(1)}, f32[256,256]{1,0:T(8,128)S(1)}, f32[256,256]{1,0:T(8,128)S(1)}) custom-call(s32[16,128]{1,0:T(8,128)S(1)} %fusion.4.refs_5_.refs_0_, s32[1]{0:T(128)} %bitcast.refs_1_.high_ref, f32[2,1168,128]{2,1,0:T(8,128)S(1)} %make_blocks.1.refs_2_, bf16[6,32,1792]{2,1,0:T(8,128)(2,1)S(1)} %pad_maximum_fusion.refs_1_.refs_3_, ...), custom_call_target="tpu_custom_call" | custom-call | flops 1000000000 | bytes 8000000 | tf_op jit(solution)/shard_map/apply_blocks/pallas_call | solution.py:290
  46.3 5.2 %collective-permute-start.5 = (f32[256,256]{1,0:T(8,128)S(1)}, f32[256,256]{1,0:T(8,128)S(1)}, u32[]{:S(2)}, u32[]{:S(2)}) collective-permute-start(f32[256,256]{1,0:T(8,128)S(1)} %get-tuple-element.16), channel_id=1, source_target_pairs={{0,4},{4,0},{8,12},{12,8},{1,5},{5,1},{9,13},{13,9},{2,6},{6,2},{1... | collective-permute-start | bytes 786440 | tf_op jit(solution)/shard_map/ppermute | solution.py:547
  51.6 1.2 %collective-permute-done.5 = f32[256,256]{1,0:T(8,128)S(1)} collective-permute-done((f32[256,256]{1,0:T(8,128)S(1)}, f32[256,256]{1,0:T(8,128)S(1)}, u32[]{:S(2)}, u32[]{:S(2)}) %collective-permute-start.5) | collective-permute-done | bytes 262176 | tf_op jit(solution)/shard_map/ppermute | solution.py:547
  52.8 0.2 collective-permute-start.6
  53.0 5.7 %collective-permute-done.6 = f32[128,256]{1,0:T(8,128)S(1)} collective-permute-done((f32[128,256]{1,0:T(8,128)S(1)}, f32[128,256]{1,0:T(8,128)S(1)}, u32[]{:S(2)}, u32[]{:S(2)}) %collective-permute-start.6) | collective-permute-done | bytes 131104 | tf_op jit(solution)/shard_map/ppermute | solution.py:477
  58.7 1.6 %collective-permute-start.7 = (f32[128,256]{1,0:T(8,128)S(1)}, f32[128,256]{1,0:T(8,128)S(1)}, u32[]{:S(2)}, u32[]{:S(2)}) collective-permute-start(f32[128,256]{1,0:T(8,128)S(1)} %select_add_fusion), channel_id=1, source_target_pairs={{0,1},{1,0},{2,3},{3,2},{4,5},{5,4},{6,7},{7,6},{8,9},{9,8},{10,11... | collective-permute-start | bytes 393224 | tf_op jit(solution)/shard_map/ppermute | solution.py:472
  60.3 3.4 %collective-permute-done.7 = f32[128,256]{1,0:T(8,128)S(1)} collective-permute-done((f32[128,256]{1,0:T(8,128)S(1)}, f32[128,256]{1,0:T(8,128)S(1)}, u32[]{:S(2)}, u32[]{:S(2)}) %collective-permute-start.7) | collective-permute-done | bytes 131104 | tf_op jit(solution)/shard_map/ppermute | solution.py:472
  63.7 2.6 %collective-permute-start.8 = (f32[128,256]{1,0:T(8,128)S(1)}, f32[128,256]{1,0:T(8,128)S(1)}, u32[]{:S(2)}, u32[]{:S(2)}) collective-permute-start(f32[128,256]{1,0:T(8,128)S(1)} %add.65), channel_id=1, source_target_pairs={{0,2},{1,3},{2,0},{3,1},{4,6},{5,7},{6,4},{7,5},{8,10},{9,11},{10,... | collective-permute-start | bytes 393224 | tf_op jit(solution)/shard_map/ppermute | solution.py:472
  66.4 4.9 %collective-permute-done.8 = f32[128,256]{1,0:T(8,128)S(1)} collective-permute-done((f32[128,256]{1,0:T(8,128)S(1)}, f32[128,256]{1,0:T(8,128)S(1)}, u32[]{:S(2)}, u32[]{:S(2)}) %collective-permute-start.8) | collective-permute-done | bytes 131104 | tf_op jit(solution)/shard_map/ppermute | solution.py:472
  71.3 1.6 %collective-permute-start.9 = (f32[128,256]{1,0:T(8,128)S(1)}, f32[128,256]{1,0:T(8,128)S(1)}, u32[]{:S(2)}, u32[]{:S(2)}) collective-permute-start(f32[128,256]{1,0:T(8,128)S(1)} %add.66), channel_id=1, source_target_pairs={{0,16},{16,0},{1,17},{17,1},{2,18},{18,2},{3,19},{19,3},{4,20},{20... | collective-permute-start | bytes 393224 | tf_op jit(solution)/shard_map/ppermute | solution.py:472
  72.9 3.4 %collective-permute-done.9 = f32[128,256]{1,0:T(8,128)S(1)} collective-permute-done((f32[128,256]{1,0:T(8,128)S(1)}, f32[128,256]{1,0:T(8,128)S(1)}, u32[]{:S(2)}, u32[]{:S(2)}) %collective-permute-start.9) | collective-permute-done | bytes 131104 | tf_op jit(solution)/shard_map/ppermute | solution.py:472
  76.3 1.0 collective-permute-start.10
  77.3 4.1 %collective-permute-done.10 = f32[128,256]{1,0:T(8,128)S(1)} collective-permute-done((f32[128,256]{1,0:T(8,128)S(1)}, f32[128,256]{1,0:T(8,128)S(1)}, u32[]{:S(2)}, u32[]{:S(2)}) %collective-permute-start.10) | collective-permute-done | bytes 131104 | tf_op jit(solution)/shard_map/ppermute | solution.py:481
  81.5 1.5 %collective-permute-done.11.got_ref = f32[256,256]{1,0:T(8,128)S(1)} collective-permute-done((f32[256,256]{1,0:T(8,128)S(1)}, f32[256,256]{1,0:T(8,128)S(1)}, u32[]{:S(2)}, u32[]{:S(2)}) %collective-permute-start.11) | collective-permute-done | bytes 262176 | tf_op jit(solution)/shard_map/ppermute | solution.py:549
  83.0 18.7 %solve.1 = (f32[128,1536]{1,0:T(8,128)}, f32[256,256]{1,0:T(8,128)}) custom-call(s32[1]{0:T(128)} %bitcast.refs_1_.high_ref, f32[256,256]{1,0:T(8,128)S(1)} %maximum_select_fusion.mine_ref, f32[256,256]{1,0:T(8,128)S(1)} %collective-permute-done.11.got_ref, f32[768,256]{1,0:T(8,128)S(1)} %get-tuple-element.17.image_ref), custom_call_target="tpu_custom_call" | custom-call | flops 1000000000 | bytes 3000000 | tf_op jit(solution)/shard_map/solve/pallas_call | solution.py:424
  (25 shorter events, 0.4 us)
Async XLA Ops:
  2.5 6.2 %collective-permute-start = (bf16[1,32,1792]{2,1,0:T(8,128)(2,1)S(1)}, bf16[1,32,1792]{2,1,0:T(8,128)(2,1)S(1)}, u32[]{:S(2)}, u32[]{:S(2)}) collective-permute-start(bf16[1,32,1792]{2,1,0:T(8,128)(2,1)S(1)} %bitcast.45), channel_id=1, source_target_pairs={{0,16},{16,0},{1,17},{17,1},{2,18},{18,2},{3,19},{19,3},{4,20},{20... | collective-permute-start | bytes 344072 | tf_op jit(solution)/shard_map/ppermute | solution.py:449
  8.7 14.6 %copy-start.4 = (s32[1,1,1,16,128]{4,3,2,1,0:T(8,128)S(1)}, s32[1,1,1,16,128]{4,3,2,1,0:T(8,128)}, u32[]{:S(2)}) copy-start(s32[1,1,1,16,128]{4,3,2,1,0:T(8,128)} %param.6) | copy-start | bytes 24580
  8.7 10.2 %collective-permute-start.1 = (bf16[2,32,1792]{2,1,0:T(8,128)(2,1)S(1)}, bf16[2,32,1792]{2,1,0:T(8,128)(2,1)S(1)}, u32[]{:S(2)}, u32[]{:S(2)}) collective-permute-start(bf16[2,32,1792]{2,1,0:T(8,128)(2,1)S(1)} %pad_maximum_fusion.1), channel_id=1, source_target_pairs={{0,1},{1,2},{2,3},{4,5},{5,6},{6,7},{8,9},{9,10},{10,11},{12,13},{... | collective-permute-start | bytes 688136 | tf_op jit(solution)/shard_map/ppermute | solution.py:450
  12.4 8.1 %collective-permute-start.2 = (bf16[2,32,1792]{2,1,0:T(8,128)(2,1)S(1)}, bf16[2,32,1792]{2,1,0:T(8,128)(2,1)S(1)}, u32[]{:S(2)}, u32[]{:S(2)}) collective-permute-start(bf16[2,32,1792]{2,1,0:T(8,128)(2,1)S(1)} %pad_maximum_fusion.1), channel_id=1, source_target_pairs={{1,0},{2,1},{3,2},{5,4},{6,5},{7,6},{9,8},{10,9},{11,10},{13,12},{... | collective-permute-start | bytes 688136 | tf_op jit(solution)/shard_map/ppermute | solution.py:450
  17.6 1.3 %copy-start.2 = (f32[2,960,256]{2,1,0:T(8,128)}, f32[2,960,256]{2,1,0:T(8,128)S(1)}, u32[]{:S(2)}) copy-start(f32[2,960,256]{2,1,0:T(8,128)S(1)} %count_pairs.2.refs_1_) | copy-start | bytes 5898244
  20.6 10.6 %collective-permute-start.3 = (bf16[6,32,1792]{2,1,0:T(8,128)(2,1)S(1)}, bf16[6,32,1792]{2,1,0:T(8,128)(2,1)S(1)}, u32[]{:S(2)}, u32[]{:S(2)}) collective-permute-start(bf16[6,32,1792]{2,1,0:T(8,128)(2,1)S(1)} %pad_maximum_fusion.refs_1_.refs_3_), channel_id=1, source_target_pairs={{0,4},{4,8},{8,12},{1,5},{5,9},{9,13},{2,6},{6,10},{10,14},{3,7},{... | collective-permute-start | bytes 2064392 | tf_op jit(solution)/shard_map/ppermute | solution.py:450
  21.9 9.2 %collective-permute-start.4 = (bf16[6,32,1792]{2,1,0:T(8,128)(2,1)S(1)}, bf16[6,32,1792]{2,1,0:T(8,128)(2,1)S(1)}, u32[]{:S(2)}, u32[]{:S(2)}) collective-permute-start(bf16[6,32,1792]{2,1,0:T(8,128)(2,1)S(1)} %pad_maximum_fusion.refs_1_.refs_3_), channel_id=1, source_target_pairs={{4,0},{8,4},{12,8},{5,1},{9,5},{13,9},{6,2},{10,6},{14,10},{7,3},{... | collective-permute-start | bytes 2064392 | tf_op jit(solution)/shard_map/ppermute | solution.py:450
  23.3 1.5 %copy-start.3 = (f32[2,960,256]{2,1,0:T(8,128)S(1)}, f32[2,960,256]{2,1,0:T(8,128)}, u32[]{:S(2)}) copy-start(f32[2,960,256]{2,1,0:T(8,128)} %copy-done.2) | copy-start | bytes 5898244
  24.9 6.3 %copy-start = (f32[1,1,1,3,16,128]{5,4,3,2,1,0:T(8,128)S(1)}, f32[1,1,1,3,16,128]{5,4,3,2,1,0:T(8,128)}, u32[]{:S(2)}) copy-start(f32[1,1,1,3,16,128]{5,4,3,2,1,0:T(8,128)} %param.5) | copy-start | bytes 73732
  31.2 6.2 %copy-start.1 = (bf16[1,1,1,128,1536]{4,3,2,1,0:T(8,128)(2,1)S(1)}, bf16[1,1,1,128,1536]{4,3,2,1,0:T(8,128)(2,1)}, u32[]{:S(2)}) copy-start(bf16[1,1,1,128,1536]{4,3,2,1,0:T(8,128)(2,1)} %param.9) | copy-start | bytes 1179652
  46.3 6.4 %collective-permute-start.5 = (f32[256,256]{1,0:T(8,128)S(1)}, f32[256,256]{1,0:T(8,128)S(1)}, u32[]{:S(2)}, u32[]{:S(2)}) collective-permute-start(f32[256,256]{1,0:T(8,128)S(1)} %get-tuple-element.16), channel_id=1, source_target_pairs={{0,4},{4,0},{8,12},{12,8},{1,5},{5,1},{9,13},{13,9},{2,6},{6,2},{1... | collective-permute-start | bytes 786440 | tf_op jit(solution)/shard_map/ppermute | solution.py:547
  52.8 5.8 %collective-permute-start.6 = (f32[128,256]{1,0:T(8,128)S(1)}, f32[128,256]{1,0:T(8,128)S(1)}, u32[]{:S(2)}, u32[]{:S(2)}) collective-permute-start(f32[128,256]{1,0:T(8,128)S(1)} %slice_select_fusion), channel_id=1, source_target_pairs={{0,8},{4,12},{8,0},{12,4},{1,9},{5,13},{9,1},{13,5},{2,10},{6,14},... | collective-permute-start | bytes 393224 | tf_op jit(solution)/shard_map/ppermute | solution.py:477
  58.7 5.0 %collective-permute-start.7 = (f32[128,256]{1,0:T(8,128)S(1)}, f32[128,256]{1,0:T(8,128)S(1)}, u32[]{:S(2)}, u32[]{:S(2)}) collective-permute-start(f32[128,256]{1,0:T(8,128)S(1)} %select_add_fusion), channel_id=1, source_target_pairs={{0,1},{1,0},{2,3},{3,2},{4,5},{5,4},{6,7},{7,6},{8,9},{9,8},{10,11... | collective-permute-start | bytes 393224 | tf_op jit(solution)/shard_map/ppermute | solution.py:472
  63.7 7.5 %collective-permute-start.8 = (f32[128,256]{1,0:T(8,128)S(1)}, f32[128,256]{1,0:T(8,128)S(1)}, u32[]{:S(2)}, u32[]{:S(2)}) collective-permute-start(f32[128,256]{1,0:T(8,128)S(1)} %add.65), channel_id=1, source_target_pairs={{0,2},{1,3},{2,0},{3,1},{4,6},{5,7},{6,4},{7,5},{8,10},{9,11},{10,... | collective-permute-start | bytes 393224 | tf_op jit(solution)/shard_map/ppermute | solution.py:472
  71.3 5.0 %collective-permute-start.9 = (f32[128,256]{1,0:T(8,128)S(1)}, f32[128,256]{1,0:T(8,128)S(1)}, u32[]{:S(2)}, u32[]{:S(2)}) collective-permute-start(f32[128,256]{1,0:T(8,128)S(1)} %add.66), channel_id=1, source_target_pairs={{0,16},{16,0},{1,17},{17,1},{2,18},{18,2},{3,19},{19,3},{4,20},{20... | collective-permute-start | bytes 393224 | tf_op jit(solution)/shard_map/ppermute | solution.py:472
  76.3 5.0 %collective-permute-start.10 = (f32[128,256]{1,0:T(8,128)S(1)}, f32[128,256]{1,0:T(8,128)S(1)}, u32[]{:S(2)}, u32[]{:S(2)}) collective-permute-start(f32[128,256]{1,0:T(8,128)S(1)} %add.67), channel_id=1, source_target_pairs={{0,8},{4,12},{8,0},{12,4},{1,9},{5,13},{9,1},{13,5},{2,10},{6,14},... | collective-permute-start | bytes 393224 | tf_op jit(solution)/shard_map/ppermute | solution.py:481
  81.4 1.6 %collective-permute-start.11 = (f32[256,256]{1,0:T(8,128)S(1)}, f32[256,256]{1,0:T(8,128)S(1)}, u32[]{:S(2)}, u32[]{:S(2)}) collective-permute-start(f32[256,256]{1,0:T(8,128)S(1)} %maximum_select_fusion.mine_ref), channel_id=1, source_target_pairs={{0,4},{4,0},{8,12},{12,8},{1,5},{5,1},{9,13},{13,9},{2,6},{6,2},{1... | collective-permute-start | bytes 786440 | tf_op jit(solution)/shard_map/ppermute | solution.py:549

commit v3 on v2

--- a/solution.py
+++ b/solution.py
@@ -23,7 +23,8 @@
 
 
 def count_kernel(*refs, frames, half, first, steps, chunk):
-    index_ref, *before, out_ref = refs
+    index_ref, *before, out_ref, done_ref = refs
+    done_ref[...] = jnp.zeros_like(done_ref)
     rows, lanes = out_ref.shape[1:]
     row_ids = lax.broadcasted_iota(jnp.int32, (rows, chunk), 0).astype(jnp.int16)
     lane_ids = lax.broadcasted_iota(jnp.int32, (lanes, chunk), 0).astype(jnp.int16)
@@ -62,8 +63,8 @@
             count_kernel, frames=frames, half=half, first=first, steps=steps, chunk=chunk
         ),
         in_specs=[vmem] * (1 + len(before)),
-        out_specs=vmem,
-        out_shape=pltpu.VMEM((2, rows, 2 * frames), f32),
+        out_specs=(vmem, vmem),
+        out_shape=(pltpu.VMEM((2, rows, 2 * frames), f32), jax.ShapeDtypeStruct((8, 128), f32)),
         cost_estimate=pl.CostEstimate(
             flops=2 * rows * 2 * frames * chunk * steps,
             bytes_accessed=rows * frames * 16,
@@ -207,7 +208,7 @@
         cost_estimate=pl.CostEstimate(flops=10**9, bytes_accessed=8 * 10**6, transcendentals=0),
         compiler_params=pltpu.CompilerParams(vmem_limit_bytes=20 << 20),
         name="make_blocks",
-    )(near_core(counts), *map(near_core, pieces), own, index)
+    )(near_core(counts), *map(near_core, pieces), near_core(own), near_core(index))
 
 
 def apply_kernel(*refs, pieces, base):
@@ -256,7 +257,7 @@
         image_scr[1, pl.ds(at, 8), :] = res[8:16]
         return carry
 
-    lax.fori_loop(0, frames, one_frame, 0, unroll=4)
+    lax.fori_loop(0, frames, one_frame, 0, unroll=32)
     dims = (((0,), (0,)), ((), ()))
     basis_gram = jnp.zeros((vectors, vectors), f32)
     cross = jnp.zeros((vectors, vectors), f32)
@@ -272,12 +273,25 @@
     cross = cross + cross.T
     rows = lax.broadcasted_iota(jnp.int32, cross.shape, 0)
     cols = lax.broadcasted_iota(jnp.int32, cross.shape, 1)
-    last = vectors - 1
-    corner = jnp.sum(jnp.where((rows == last) & (cols == last), cross, 0.0), axis=0, keepdims=True)
-    diag = jnp.where((rows == cols) & (rows < last), cross, 0.0)
-    diag = pltpu.roll(diag, 1, 1) + jnp.where(rows == 0, corner, 0.0)
-    front = jnp.where(rows >= cols, image_gram, cross)
-    back = jnp.where(rows >= cols, basis_gram, diag)
+    part = vectors // 2
+    diag = jnp.sum(jnp.where(rows == cols, cross, 0.0), axis=0, keepdims=True)
+    low = basis_gram[part:, part:].T
+    edge = rows[0:part, 0:part] == cols[0:part, 0:part]
+    low_diag = jnp.sum(jnp.where(edge, low, 0.0), axis=0, keepdims=True)
+    square = jnp.where(rows[0:part, 0:part] >= cols[0:part, 0:part], basis_gram[0:part, 0:part], low)
+    mixed = jnp.where(rows >= cols, image_gram, cross)
+    cut = keep_ref.shape[0]
+    front = mixed[0:cut]
+    back = jnp.concatenate(
+        [
+            mixed[cut:],
+            jnp.concatenate([square, basis_gram[part:, 0:part]], axis=1),
+            jnp.broadcast_to(diag, (8, vectors)),
+            jnp.broadcast_to(jnp.concatenate([low_diag, low_diag], axis=1), (8, vectors)),
+            jnp.zeros((2 * cut - 3 * part - 16, vectors), f32),
+        ],
+        axis=0,
+    )
     high = high_ref[0] != 0
     keep_ref[...] = jnp.where(high, back, front)
     send_ref[...] = jnp.where(high, front, back)
@@ -286,6 +300,7 @@
 def apply_blocks(index, high, coeff, pieces, own, base):
     slots, frames = index.shape
     vectors = own.shape[1] // 6
+    cut = round_up(3 * vectors // 2 + 16, 32) // 2
     vmem = pl.BlockSpec(memory_space=pltpu.VMEM)
     return pl.pallas_call(
         functools.partial(apply_kernel, pieces=len(pieces), base=base),
@@ -293,8 +308,8 @@
         out_specs=(vmem, vmem, vmem),
         out_shape=(
             pltpu.VMEM((frames * 6, vectors), f32),
-            pltpu.VMEM((vectors, vectors), f32),
-            pltpu.VMEM((vectors, vectors), f32),
+            pltpu.VMEM((cut, vectors), f32),
+            pltpu.VMEM((cut, vectors), f32),
         ),
         scratch_shapes=[
             pltpu.VMEM(((base + frames) * (own.shape[1] // 128 + 1) + 16, 128), f32),
@@ -303,36 +318,39 @@
         cost_estimate=pl.CostEstimate(flops=10**9, bytes_accessed=8 * 10**6, transcendentals=0),
         compiler_params=pltpu.CompilerParams(vmem_limit_bytes=24 << 20),
         name="apply_blocks",
-    )(index, high, near_core(coeff), *map(near_core, pieces), own)
-
-
-panel = 64
+    )(index, high, near_core(coeff), *map(near_core, pieces), near_core(own))
+
+
+panel = 128
 
 
 def factor_panels(blocks):
     groups = panel // 8
     sub = lax.broadcasted_iota(jnp.int32, (8, 128), 0)
     every = range(len(blocks))
-    rows = [[block[g * 8 : (g + 1) * 8] for g in range(groups)] for block in blocks]
+    tiles = range(2)
+    rows = [[[t[g * 8 : (g + 1) * 8] for t in block] for g in range(groups)] for block in blocks]
 
     def spread_row(x, k):
         return jnp.broadcast_to(x[k : k + 1, :], (8, 128))
 
+    def columns(b, r, g):
+        return [jnp.broadcast_to(rows[b][r][0][:, g * 8 + k : g * 8 + k + 1], (8, 128)) for k in range(8)]
+
+    def update(b, r, cols, gain):
+        for t in tiles:
+            for k in range(8):
+                rows[b][r][t] = rows[b][r][t] - cols[k] * gain[b][t][k]
+
     for g in range(groups):
-        wide = [
-            [
-                [jnp.broadcast_to(rows[b][r][:, g * 8 + k : g * 8 + k + 1], (8, 128)) for k in range(8)]
-                for r in range(g, groups)
-            ]
-            for b in every
-        ]
-        top = [rows[b][g] for b in every]
-        full = list(top)
+        leads = [columns(b, g, g) for b in every]
+        top = [list(rows[b][g]) for b in every]
+        full = [list(rows[b][g]) for b in every]
         scale = [jnp.zeros((8, 128), f32) for b in every]
         square = [jnp.zeros((8, 128), f32) for b in every]
         for k in range(8):
             for b in every:
-                lead = wide[b][0]
+                lead = leads[b]
                 root = lax.rsqrt(spread_row(lead[k], k))
                 inv = root * root
                 scale[b] = jnp.where(sub == k, root, scale[b])
@@ -341,20 +359,17 @@
                 below = jnp.where(sub > k, factor, 0.0)
                 for m in range(k + 1, 8):
                     lead[m] = lead[m] - factor * spread_row(lead[m], k)
-                top[b] = top[b] - below * spread_row(top[b], k)
-                full[b] = full[b] - factor * spread_row(full[b], k)
+                for t in tiles:
+                    top[b][t] = top[b][t] - below * spread_row(top[b][t], k)
+                    full[b][t] = full[b][t] - factor * spread_row(full[b][t], k)
+        gain = [[x * square[b] for x in full[b]] for b in every]
+        gain = [[[spread_row(x, k) for k in range(8)] for x in gain[b]] for b in every]
         for b in every:
-            gain = full[b] * square[b]
-            gain = [spread_row(gain, k) for k in range(8)]
             for r in range(g + 1, groups):
-                row = rows[b][r]
-                cols = wide[b][r - g]
-                for k in range(8):
-                    row = row - cols[k] * gain[k]
-                rows[b][r] = row
+                update(b, r, columns(b, r, g), gain)
         for b in every:
-            rows[b][g] = top[b] * scale[b]
-    return [jnp.concatenate(rows[b], axis=0) for b in every]
+            rows[b][g] = [x * scale[b] for x in top[b]]
+    return [jnp.concatenate([rows[b][g][1] for g in range(groups)], axis=0) for b in every]
 
 
 def solve_kernel(high_ref, mine_ref, got_ref, image_ref, next_ref, ritz_ref, image_scr, basis_scr, *, total_rows):
@@ -365,15 +380,26 @@
     high = high_ref[0] != 0
     mine = mine_ref[...] * (1.0 / total_rows)
     got = got_ref[...] * (1.0 / total_rows)
-    mixed = jnp.where(high, got, mine)
-    other = jnp.where(high, mine, got)
+    cut = mine.shape[0]
+    part = size // 2
+    front = jnp.where(high, got, mine)
+    back = jnp.where(high, mine, got)
+    mixed = jnp.concatenate([front, back[0 : size - cut]], axis=0)
+    at = size - cut
+    square = back[at : at + part, 0:part]
+    side = back[at : at + part, part:]
+    at += part
+    diag = back[at : at + 1]
+    low_diag = back[at + 8 : at + 9, 0:part]
     turned = mixed.T
+    square_t = square.T
     image_gram = jnp.where(rows >= cols, mixed, turned)
-    basis_gram = jnp.where(rows >= cols, other, other.T)
-    last = size - 1
-    diag = pltpu.roll(jnp.where(cols == rows + 1, other, 0.0), size - 1, 1)
-    corner = jnp.sum(jnp.where((rows == 0) & (cols == last), other, 0.0), axis=0, keepdims=True)
-    diag = diag + jnp.where(rows == last, corner, 0.0)
+    r, c = rows[0:part, 0:part], cols[0:part, 0:part]
+    first = jnp.where(r >= c, square, square_t)
+    second = jnp.where(r < c, square, jnp.where(r > c, square_t, low_diag))
+    basis_gram = jnp.concatenate(
+        [jnp.concatenate([first, side.T], axis=1), jnp.concatenate([side, second], axis=1)], axis=0
+    )
     cross = jnp.where(rows < cols, mixed, jnp.where(rows > cols, turned, diag)) * 0.5
     eye = jnp.where(rows == cols, 1.0, 0.0)
     scratch = (image_scr, basis_scr)
@@ -387,26 +413,21 @@
         1.0,
         0.0,
     )
-    lane_ids = lax.broadcasted_iota(jnp.int32, (panel, size), 1)
-
-    def one_panel(p, carry):
-        at = pl.multiple_of(p * panel, panel)
-        strips = [ref[pl.ds(at, panel), :] for ref in scratch]
-        fronts = [pltpu.roll(x[:, 0:size], size - at, 1)[:, 0:panel] for x in strips]
-        solved = factor_panels([jnp.concatenate([x, small], axis=1) for x in fronts])
+
+    for at in range(0, size, panel):
+        strips = [ref[at : at + panel, :] for ref in scratch]
+        solved = factor_panels([(x[:, at : at + panel], small) for x in strips])
         done = [
-            jnp.dot(inv[:, panel:], x, precision=exact, preferred_element_type=f32)
+            jnp.dot(inv, x, precision=exact, preferred_element_type=f32)
             for inv, x in zip(solved, strips)
         ]
         for ref, x in zip(scratch, done):
-            left = jnp.where(lane_ids >= at + panel, x[:, 0:size], 0.0)
-            ref[...] = ref[...] - lax.dot_general(
-                left, x, (((0,), (0,)), ((), ())), precision=exact, preferred_element_type=f32
-            )
-            ref[pl.ds(at, panel), :] = x
-        return carry
-
-    lax.fori_loop(0, size // panel, one_panel, 0)
+            ref[at : at + panel, :] = x
+            for r in range(at + panel, size, panel):
+                left = x[:, r : r + panel]
+                ref[r : r + panel, :] = ref[r : r + panel, :] - lax.dot_general(
+                    left, x, (((0,), (0,)), ((), ())), precision=exact, preferred_element_type=f32
+                )
     image_inv = image_scr[:, size:]
     basis_inv = basis_scr[:, size:]
     turn = (((1,), (1,)), ((), ()))
@@ -533,11 +554,11 @@
     )
     part = jnp.concatenate(spread(row[None], "gx"), axis=0)
     table, part = lax.optimization_barrier((table, part))
-    counts = count_pairs([], table, frames, slots, atoms, cut[0], cut[1] - cut[0], chunk)
+    counts, done = count_pairs([], table, frames, slots, atoms, cut[0], cut[1] - cut[0], chunk)
     part = jnp.concatenate(spread(part, "gz"), axis=0)
-    counts, part = lax.optimization_barrier((counts, part))
+    part = part + done[0, 0].astype(bf16)
     near = spread(part, "gy")
-    counts = count_pairs([counts], table, frames, slots, atoms, cut[1], cut[2] - cut[1], chunk)
+    counts, done = count_pairs([counts], table, frames, slots, atoms, cut[1], cut[2] - cut[1], chunk)
     coeff = make_blocks(counts, near, own_coords, index, base, columns)
     axis = "gy"
     pairs = [(i, i ^ 1) for i in range(lax.axis_size(axis))]

time: 102 us -> 91.9 us (0.901)
  Pallas kernels: 44 us -> 37.1 us
  waiting for transfers between devices: 27.8 us -> 21.2 us
  starting transfers between devices: 23 us -> 25.1 us
    ppermute x1, starting transfers between devices: 5.25 us -> 1.37 us  [per_device(): mine = keep + lax.ppermute(send, axis, pairs)]
    pallas_call x1, Pallas kernels: 18.7 us -> 14.9 us  [solve(): pl.pallas_call(functools.partial(solve_kernel, total_rows=float(total_row...]
    pallas_call x1, Pallas kernels: 8.96 us -> 5.89 us  [apply_blocks(): pl.pallas_call(functools.partial(apply_kernel, pieces=len(pieces), base=b...]
    ppermute x2, starting transfers between devices: 5.05 us -> 7.63 us  [spread(): lax.ppermute(stack, axis, up)]
    ppermute x1, starting transfers between devices: 0.16 us -> 2.69 us  [sum_all(): got = lax.ppermute(jnp.where(high, front, back), axis, pairs)]
    ppermute x1, waiting for transfers between devices: 5.68 us -> 3.27 us  [sum_all(): got = lax.ppermute(jnp.where(high, front, back), axis, pairs)]
    ppermute x2, waiting for transfers between devices: 1.66 us -> 0.01 us  [spread(): lax.ppermute(stack, axis, down)]
    ppermute x3, waiting for transfers between devices: 11.8 us -> 10.5 us  [sum_all(): values = values + lax.ppermute(values, axis, pairs)]
  transfers between devices with their start and end apart: 12 -> 12, of which waited for: 9 -> 8; matrix products, arithmetic and copies ran while one was open for 1% -> 2% of each run, Pallas kernels for 10% -> 11%
where the time goes in v3:
time: 91.9 us; the launch traced here: 91.5 us
  Pallas kernels  37.1 us (40%)
  starting transfers between devices  25.1 us (27%)
  waiting for transfers between devices  21.2 us (23%)
  local copies, waits for them, and re-layouts  5.23 us (6%)
  other arithmetic  2.02 us (2%)
    pallas_call x1, Pallas kernels, solve(): pl.pallas_call(functools.partial(solve_kernel, total_rows=float(total_row...  14.9 us
    ppermute x3, waiting for transfers between devices, sum_all(): values = values + lax.ppermute(values, axis, pairs)  10.5 us
    pallas_call x2, Pallas kernels, count_pairs(): pl.pallas_call(functools.partial(count_kernel, frames=frames, half=half,...  10.1 us
    ppermute x2, starting transfers between devices, spread(): lax.ppermute(stack, axis, up)  7.63 us
    pallas_call x1, Pallas kernels, make_blocks(): pl.pallas_call(functools.partial(block_kernel, pieces=len(pieces), base=b...  6.14 us
    pallas_call x1, Pallas kernels, apply_blocks(): pl.pallas_call(functools.partial(apply_kernel, pieces=len(pieces), base=b...  5.89 us
    ppermute x3, starting transfers between devices, sum_all(): values = values + lax.ppermute(values, axis, pairs)  5.86 us
    unnamed x11, local copies, waits for them, and re-layouts  3.64 us
  transfers between devices with their start and end apart: 12, of which 8 were waited for; matrix products, arithmetic and copies ran while one was open for 2% of the time, Pallas kernels for 11%

profile of v3, /device:TPU:0, one launch (start us, length us, event | category | flops | bytes accessed | tf_op | source)
XLA Modules:
  0.0 91.5 jit_solution(16260924129051971129)
XLA Ops:
  0.6 0.8 copy.9
  1.5 0.9 slice_bitcast_fusion
  2.4 0.1 concatenate.19
  2.5 3.1 %collective-permute-start = (bf16[1,32,1792]{2,1,0:T(8,128)(2,1)S(1)}, bf16[1,32,1792]{2,1,0:T(8,128)(2,1)S(1)}, u32[]{:S(2)}, u32[]{:S(2)}) collective-permute-start(bf16[1,32,1792]{2,1,0:T(8,128)(2,1)S(1)} %bitcast.46), channel_id=1, source_target_pairs={{0,16},{16,0},{1,17},{17,1},{2,18},{18,2},{3,19},{19,3},{4,20},{20... | collective-permute-start | bytes 344072 | tf_op jit(solution)/shard_map/ppermute | solution.py:470
  5.6 1.1 %add_add_fusion.refs_0_ = s32[8,15360]{1,0:T(8,128)S(1)} fusion(s32[1,15360]{1,0:T(1,128)} %bitcast.49, s32[4,15360]{1,0:T(4,128)} %bitcast.48, s32[8]{0:T(128)S(1)} %pad.11.clone), kind=kLoop, calls=%fused_computation.1 | loop fusion | flops 245760 | bytes 798752 | tf_op jit(solution)/shard_map/concatenate | solution.py:552
  6.7 2.0 %collective-permute-done = bf16[1,32,1792]{2,1,0:T(8,128)(2,1)S(1)} collective-permute-done((bf16[1,32,1792]{2,1,0:T(8,128)(2,1)S(1)}, bf16[1,32,1792]{2,1,0:T(8,128)(2,1)S(1)}, u32[]{:S(2)}, u32[]{:S(2)}) %collective-permute-start) | collective-permute-done | bytes 114720 | tf_op jit(solution)/shard_map/ppermute | solution.py:470
  8.7 1.3 %collective-permute-start.2 = (bf16[2,32,1792]{2,1,0:T(8,128)(2,1)S(1)}, bf16[2,32,1792]{2,1,0:T(8,128)(2,1)S(1)}, u32[]{:S(2)}, u32[]{:S(2)}) collective-permute-start(bf16[2,32,1792]{2,1,0:T(8,128)(2,1)S(1)} %pad_maximum_fusion), channel_id=1, source_target_pairs={{1,0},{2,1},{3,2},{5,4},{6,5},{7,6},{9,8},{10,9},{11,10},{13,12},{... | collective-permute-start | bytes 688136 | tf_op jit(solution)/shard_map/ppermute | solution.py:471
  10.0 4.6 %collective-permute-start.1 = (bf16[2,32,1792]{2,1,0:T(8,128)(2,1)S(1)}, bf16[2,32,1792]{2,1,0:T(8,128)(2,1)S(1)}, u32[]{:S(2)}, u32[]{:S(2)}) collective-permute-start(bf16[2,32,1792]{2,1,0:T(8,128)(2,1)S(1)} %pad_maximum_fusion), channel_id=1, source_target_pairs={{0,1},{1,2},{2,3},{4,5},{5,6},{6,7},{8,9},{9,10},{10,11},{12,13},{... | collective-permute-start | bytes 688136 | tf_op jit(solution)/shard_map/ppermute | solution.py:471
  14.6 3.9 %count_pairs.2 = (f32[2,960,256]{2,1,0:T(8,128)S(1)}, f32[8,128]{1,0:T(8,128)S(1)}) custom-call(s32[8,15360]{1,0:T(8,128)S(1)} %add_add_fusion.refs_0_), custom_call_target="tpu_custom_call" | custom-call | flops 2831155200 | bytes 1966080 | tf_op jit(solution)/shard_map/count_pairs/pallas_call | solution.py:61
  18.4 1.3 %copy-done.2 = f32[2,960,256]{2,1,0:T(8,128)} copy-done((f32[2,960,256]{2,1,0:T(8,128)}, f32[2,960,256]{2,1,0:T(8,128)S(1)}, u32[]{:S(2)}) %copy-start.2) | copy-done | bytes 1966104
  19.7 0.5 slice.22
  20.2 0.7 maximum_add_fusion.refs_1_.refs_3_
  21.0 1.3 %collective-permute-start.4 = (bf16[6,32,1792]{2,1,0:T(8,128)(2,1)S(1)}, bf16[6,32,1792]{2,1,0:T(8,128)(2,1)S(1)}, u32[]{:S(2)}, u32[]{:S(2)}) collective-permute-start(bf16[6,32,1792]{2,1,0:T(8,128)(2,1)S(1)} %maximum_add_fusion.refs_1_.refs_3_), channel_id=1, source_target_pairs={{4,0},{8,4},{12,8},{5,1},{9,5},{13,9},{6,2},{10,6},{14,10},{7,3},{... | collective-permute-start | bytes 2064392 | tf_op jit(solution)/shard_map/ppermute | solution.py:471
  22.3 3.1 %collective-permute-start.3 = (bf16[6,32,1792]{2,1,0:T(8,128)(2,1)S(1)}, bf16[6,32,1792]{2,1,0:T(8,128)(2,1)S(1)}, u32[]{:S(2)}, u32[]{:S(2)}) collective-permute-start(bf16[6,32,1792]{2,1,0:T(8,128)(2,1)S(1)} %maximum_add_fusion.refs_1_.refs_3_), channel_id=1, source_target_pairs={{0,4},{4,8},{8,12},{1,5},{5,9},{9,13},{2,6},{6,10},{10,14},{3,7},{... | collective-permute-start | bytes 2064392 | tf_op jit(solution)/shard_map/ppermute | solution.py:471
  25.4 1.5 %copy-done.3 = f32[2,960,256]{2,1,0:T(8,128)S(1)} copy-done((f32[2,960,256]{2,1,0:T(8,128)S(1)}, f32[2,960,256]{2,1,0:T(8,128)}, u32[]{:S(2)}) %copy-start.3) | copy-done | bytes 1966104
  27.0 6.3 %count_pairs.3 = (f32[2,960,256]{2,1,0:T(8,128)S(1)}, f32[8,128]{1,0:T(8,128)}) custom-call(s32[8,15360]{1,0:T(8,128)S(1)} %add_add_fusion.refs_0_, f32[2,960,256]{2,1,0:T(8,128)S(1)} %copy-done.3), custom_call_target="tpu_custom_call" | custom-call | flops 4718592000 | bytes 1966080 | tf_op jit(solution)/shard_map/count_pairs/pallas_call | solution.py:61
  33.3 6.1 %make_blocks.1.refs_2_ = f32[2,1168,128]{2,1,0:T(8,128)S(1)} custom-call(f32[2,960,256]{2,1,0:T(8,128)S(1)} %get-tuple-element.14.refs_0_, bf16[6,32,1792]{2,1,0:T(8,128)(2,1)S(1)} %maximum_add_fusion.refs_1_.refs_3_, bf16[6,32,1792]{2,1,0:T(8,128)(2,1)S(1)} %collective-permute-done.3.refs_2_.refs_4_, ...), custom_call_target="tpu_custom_call" | custom-call | flops 1000000000 | bytes 8000000 | tf_op jit(solution)/shard_map/make_blocks/pallas_call | solution.py:197
  39.5 5.9 %apply_blocks.1 = (f32[768,256]{1,0:T(8,128)S(1)}, f32[208,256]{1,0:T(8,128)S(1)}, f32[208,256]{1,0:T(8,128)S(1)}) custom-call(s32[16,128]{1,0:T(8,128)S(1)} %fusion.4.refs_5_.refs_0_, s32[1]{0:T(128)} %bitcast.refs_1_.high_ref, f32[2,1168,128]{2,1,0:T(8,128)S(1)} %make_blocks.1.refs_2_, bf16[6,32,1792]{2,1,0:T(8,128)(2,1)S(1)} %maximum_add_fusion.refs_1_.refs_3_, ...), custom_call_target="tpu_custom_call" | custom-call | flops 1000000000 | bytes 8000000 | tf_op jit(solution)/shard_map/apply_blocks/pallas_call | solution.py:305
  45.4 1.4 %collective-permute-start.5 = (f32[208,256]{1,0:T(8,128)S(1)}, f32[208,256]{1,0:T(8,128)S(1)}, u32[]{:S(2)}, u32[]{:S(2)}) collective-permute-start(f32[208,256]{1,0:T(8,128)S(1)} %get-tuple-element.18), channel_id=1, source_target_pairs={{0,4},{4,0},{8,12},{12,8},{1,5},{5,1},{9,13},{13,9},{2,6},{6,2},{1... | collective-permute-start | bytes 638984 | tf_op jit(solution)/shard_map/ppermute | solution.py:568
  46.7 1.1 %collective-permute-done.5 = f32[208,256]{1,0:T(8,128)S(1)} collective-permute-done((f32[208,256]{1,0:T(8,128)S(1)}, f32[208,256]{1,0:T(8,128)S(1)}, u32[]{:S(2)}, u32[]{:S(2)}) %collective-permute-start.5) | collective-permute-done | bytes 213024 | tf_op jit(solution)/shard_map/ppermute | solution.py:568
  47.9 2.7 %collective-permute-start.6 = (f32[104,256]{1,0:T(8,128)S(1)}, f32[104,256]{1,0:T(8,128)S(1)}, u32[]{:S(2)}, u32[]{:S(2)}) collective-permute-start(f32[104,256]{1,0:T(8,128)S(1)} %slice_select_fusion), channel_id=1, source_target_pairs={{0,8},{4,12},{8,0},{12,4},{1,9},{5,13},{9,1},{13,5},{2,10},{6,14},... | collective-permute-start | bytes 319496 | tf_op jit(solution)/shard_map/ppermute | solution.py:498
  50.6 3.3 %collective-permute-done.6 = f32[104,256]{1,0:T(8,128)S(1)} collective-permute-done((f32[104,256]{1,0:T(8,128)S(1)}, f32[104,256]{1,0:T(8,128)S(1)}, u32[]{:S(2)}, u32[]{:S(2)}) %collective-permute-start.6) | collective-permute-done | bytes 106528 | tf_op jit(solution)/shard_map/ppermute | solution.py:498
  53.9 1.6 %collective-permute-start.7 = (f32[104,256]{1,0:T(8,128)S(1)}, f32[104,256]{1,0:T(8,128)S(1)}, u32[]{:S(2)}, u32[]{:S(2)}) collective-permute-start(f32[104,256]{1,0:T(8,128)S(1)} %select_add_fusion), channel_id=1, source_target_pairs={{0,1},{1,0},{2,3},{3,2},{4,5},{5,4},{6,7},{7,6},{8,9},{9,8},{10,11... | collective-permute-start | bytes 319496 | tf_op jit(solution)/shard_map/ppermute | solution.py:493
  55.5 3.1 %collective-permute-done.7 = f32[104,256]{1,0:T(8,128)S(1)} collective-permute-done((f32[104,256]{1,0:T(8,128)S(1)}, f32[104,256]{1,0:T(8,128)S(1)}, u32[]{:S(2)}, u32[]{:S(2)}) %collective-permute-start.7) | collective-permute-done | bytes 106528 | tf_op jit(solution)/shard_map/ppermute | solution.py:493
  58.7 2.7 %collective-permute-start.8 = (f32[104,256]{1,0:T(8,128)S(1)}, f32[104,256]{1,0:T(8,128)S(1)}, u32[]{:S(2)}, u32[]{:S(2)}) collective-permute-start(f32[104,256]{1,0:T(8,128)S(1)} %add.73), channel_id=1, source_target_pairs={{0,2},{1,3},{2,0},{3,1},{4,6},{5,7},{6,4},{7,5},{8,10},{9,11},{10,... | collective-permute-start | bytes 319496 | tf_op jit(solution)/shard_map/ppermute | solution.py:493
  61.3 4.2 %collective-permute-done.8 = f32[104,256]{1,0:T(8,128)S(1)} collective-permute-done((f32[104,256]{1,0:T(8,128)S(1)}, f32[104,256]{1,0:T(8,128)S(1)}, u32[]{:S(2)}, u32[]{:S(2)}) %collective-permute-start.8) | collective-permute-done | bytes 106528 | tf_op jit(solution)/shard_map/ppermute | solution.py:493
  65.5 1.6 %collective-permute-start.9 = (f32[104,256]{1,0:T(8,128)S(1)}, f32[104,256]{1,0:T(8,128)S(1)}, u32[]{:S(2)}, u32[]{:S(2)}) collective-permute-start(f32[104,256]{1,0:T(8,128)S(1)} %add.74), channel_id=1, source_target_pairs={{0,16},{16,0},{1,17},{17,1},{2,18},{18,2},{3,19},{19,3},{4,20},{20... | collective-permute-start | bytes 319496 | tf_op jit(solution)/shard_map/ppermute | solution.py:493
  67.1 3.2 %collective-permute-done.9 = f32[104,256]{1,0:T(8,128)S(1)} collective-permute-done((f32[104,256]{1,0:T(8,128)S(1)}, f32[104,256]{1,0:T(8,128)S(1)}, u32[]{:S(2)}, u32[]{:S(2)}) %collective-permute-start.9) | collective-permute-done | bytes 106528 | tf_op jit(solution)/shard_map/ppermute | solution.py:493
  70.3 1.8 %collective-permute-start.10 = (f32[104,256]{1,0:T(8,128)S(1)}, f32[104,256]{1,0:T(8,128)S(1)}, u32[]{:S(2)}, u32[]{:S(2)}) collective-permute-start(f32[104,256]{1,0:T(8,128)S(1)} %add.75), channel_id=1, source_target_pairs={{0,8},{4,12},{8,0},{12,4},{1,9},{5,13},{9,1},{13,5},{2,10},{6,14},... | collective-permute-start | bytes 319496 | tf_op jit(solution)/shard_map/ppermute | solution.py:502
  72.1 3.0 %collective-permute-done.10 = f32[104,256]{1,0:T(8,128)S(1)} collective-permute-done((f32[104,256]{1,0:T(8,128)S(1)}, f32[104,256]{1,0:T(8,128)S(1)}, u32[]{:S(2)}, u32[]{:S(2)}) %collective-permute-start.10) | collective-permute-done | bytes 106528 | tf_op jit(solution)/shard_map/ppermute | solution.py:502
  75.1 1.5 %collective-permute-done.11.got_ref = f32[208,256]{1,0:T(8,128)S(1)} collective-permute-done((f32[208,256]{1,0:T(8,128)S(1)}, f32[208,256]{1,0:T(8,128)S(1)}, u32[]{:S(2)}, u32[]{:S(2)}) %collective-permute-start.11) | collective-permute-done | bytes 213024 | tf_op jit(solution)/shard_map/ppermute | solution.py:570
  76.6 14.9 %solve.1 = (f32[128,1536]{1,0:T(8,128)}, f32[256,256]{1,0:T(8,128)}) custom-call(s32[1]{0:T(128)} %bitcast.refs_1_.high_ref, f32[208,256]{1,0:T(8,128)S(1)} %maximum_select_fusion.mine_ref, f32[208,256]{1,0:T(8,128)S(1)} %collective-permute-done.11.got_ref, f32[768,256]{1,0:T(8,128)S(1)} %get-tuple-element.19.image_ref), custom_call_target="tpu_custom_call" | custom-call | flops 1000000000 | bytes 3000000 | tf_op jit(solution)/shard_map/solve/pallas_call | solution.py:445
  (27 shorter events, 0.4 us)
Async XLA Ops:
  2.5 6.2 %collective-permute-start = (bf16[1,32,1792]{2,1,0:T(8,128)(2,1)S(1)}, bf16[1,32,1792]{2,1,0:T(8,128)(2,1)S(1)}, u32[]{:S(2)}, u32[]{:S(2)}) collective-permute-start(bf16[1,32,1792]{2,1,0:T(8,128)(2,1)S(1)} %bitcast.46), channel_id=1, source_target_pairs={{0,16},{16,0},{1,17},{17,1},{2,18},{18,2},{3,19},{19,3},{4,20},{20... | collective-permute-start | bytes 344072 | tf_op jit(solution)/shard_map/ppermute | solution.py:470
  8.7 16.7 %copy-start.4 = (s32[1,1,1,16,128]{4,3,2,1,0:T(8,128)S(1)}, s32[1,1,1,16,128]{4,3,2,1,0:T(8,128)}, u32[]{:S(2)}) copy-start(s32[1,1,1,16,128]{4,3,2,1,0:T(8,128)} %param.6) | copy-start | bytes 24580
  8.7 11.5 %collective-permute-start.2 = (bf16[2,32,1792]{2,1,0:T(8,128)(2,1)S(1)}, bf16[2,32,1792]{2,1,0:T(8,128)(2,1)S(1)}, u32[]{:S(2)}, u32[]{:S(2)}) collective-permute-start(bf16[2,32,1792]{2,1,0:T(8,128)(2,1)S(1)} %pad_maximum_fusion), channel_id=1, source_target_pairs={{1,0},{2,1},{3,2},{5,4},{6,5},{7,6},{9,8},{10,9},{11,10},{13,12},{... | collective-permute-start | bytes 688136 | tf_op jit(solution)/shard_map/ppermute | solution.py:471
  10.0 10.2 %collective-permute-start.1 = (bf16[2,32,1792]{2,1,0:T(8,128)(2,1)S(1)}, bf16[2,32,1792]{2,1,0:T(8,128)(2,1)S(1)}, u32[]{:S(2)}, u32[]{:S(2)}) collective-permute-start(bf16[2,32,1792]{2,1,0:T(8,128)(2,1)S(1)} %pad_maximum_fusion), channel_id=1, source_target_pairs={{0,1},{1,2},{2,3},{4,5},{5,6},{6,7},{8,9},{9,10},{10,11},{12,13},{... | collective-permute-start | bytes 688136 | tf_op jit(solution)/shard_map/ppermute | solution.py:471
  18.4 1.3 %copy-start.2 = (f32[2,960,256]{2,1,0:T(8,128)}, f32[2,960,256]{2,1,0:T(8,128)S(1)}, u32[]{:S(2)}) copy-start(f32[2,960,256]{2,1,0:T(8,128)S(1)} %get-tuple-element.13.refs_1_) | copy-start | bytes 5898244
  21.0 12.3 %collective-permute-start.4 = (bf16[6,32,1792]{2,1,0:T(8,128)(2,1)S(1)}, bf16[6,32,1792]{2,1,0:T(8,128)(2,1)S(1)}, u32[]{:S(2)}, u32[]{:S(2)}) collective-permute-start(bf16[6,32,1792]{2,1,0:T(8,128)(2,1)S(1)} %maximum_add_fusion.refs_1_.refs_3_), channel_id=1, source_target_pairs={{4,0},{8,4},{12,8},{5,1},{9,5},{13,9},{6,2},{10,6},{14,10},{7,3},{... | collective-permute-start | bytes 2064392 | tf_op jit(solution)/shard_map/ppermute | solution.py:471
  22.3 11.0 %collective-permute-start.3 = (bf16[6,32,1792]{2,1,0:T(8,128)(2,1)S(1)}, bf16[6,32,1792]{2,1,0:T(8,128)(2,1)S(1)}, u32[]{:S(2)}, u32[]{:S(2)}) collective-permute-start(bf16[6,32,1792]{2,1,0:T(8,128)(2,1)S(1)} %maximum_add_fusion.refs_1_.refs_3_), channel_id=1, source_target_pairs={{0,4},{4,8},{8,12},{1,5},{5,9},{9,13},{2,6},{6,10},{10,14},{3,7},{... | collective-permute-start | bytes 2064392 | tf_op jit(solution)/shard_map/ppermute | solution.py:471
  25.4 1.5 %copy-start.3 = (f32[2,960,256]{2,1,0:T(8,128)S(1)}, f32[2,960,256]{2,1,0:T(8,128)}, u32[]{:S(2)}) copy-start(f32[2,960,256]{2,1,0:T(8,128)} %copy-done.2) | copy-start | bytes 5898244
  27.0 6.3 %copy-start = (f32[1,1,1,3,16,128]{5,4,3,2,1,0:T(8,128)S(1)}, f32[1,1,1,3,16,128]{5,4,3,2,1,0:T(8,128)}, u32[]{:S(2)}) copy-start(f32[1,1,1,3,16,128]{5,4,3,2,1,0:T(8,128)} %param.5) | copy-start | bytes 73732
  33.3 6.2 %copy-start.1 = (bf16[1,1,1,128,1536]{4,3,2,1,0:T(8,128)(2,1)S(1)}, bf16[1,1,1,128,1536]{4,3,2,1,0:T(8,128)(2,1)}, u32[]{:S(2)}) copy-start(bf16[1,1,1,128,1536]{4,3,2,1,0:T(8,128)(2,1)} %param.9) | copy-start | bytes 1179652
  45.4 2.5 %collective-permute-start.5 = (f32[208,256]{1,0:T(8,128)S(1)}, f32[208,256]{1,0:T(8,128)S(1)}, u32[]{:S(2)}, u32[]{:S(2)}) collective-permute-start(f32[208,256]{1,0:T(8,128)S(1)} %get-tuple-element.18), channel_id=1, source_target_pairs={{0,4},{4,0},{8,12},{12,8},{1,5},{5,1},{9,13},{13,9},{2,6},{6,2},{1... | collective-permute-start | bytes 638984 | tf_op jit(solution)/shard_map/ppermute | solution.py:568
  47.9 6.0 %collective-permute-start.6 = (f32[104,256]{1,0:T(8,128)S(1)}, f32[104,256]{1,0:T(8,128)S(1)}, u32[]{:S(2)}, u32[]{:S(2)}) collective-permute-start(f32[104,256]{1,0:T(8,128)S(1)} %slice_select_fusion), channel_id=1, source_target_pairs={{0,8},{4,12},{8,0},{12,4},{1,9},{5,13},{9,1},{13,5},{2,10},{6,14},... | collective-permute-start | bytes 319496 | tf_op jit(solution)/shard_map/ppermute | solution.py:498
  53.9 4.8 %collective-permute-start.7 = (f32[104,256]{1,0:T(8,128)S(1)}, f32[104,256]{1,0:T(8,128)S(1)}, u32[]{:S(2)}, u32[]{:S(2)}) collective-permute-start(f32[104,256]{1,0:T(8,128)S(1)} %select_add_fusion), channel_id=1, source_target_pairs={{0,1},{1,0},{2,3},{3,2},{4,5},{5,4},{6,7},{7,6},{8,9},{9,8},{10,11... | collective-permute-start | bytes 319496 | tf_op jit(solution)/shard_map/ppermute | solution.py:493
  58.7 6.8 %collective-permute-start.8 = (f32[104,256]{1,0:T(8,128)S(1)}, f32[104,256]{1,0:T(8,128)S(1)}, u32[]{:S(2)}, u32[]{:S(2)}) collective-permute-start(f32[104,256]{1,0:T(8,128)S(1)} %add.73), channel_id=1, source_target_pairs={{0,2},{1,3},{2,0},{3,1},{4,6},{5,7},{6,4},{7,5},{8,10},{9,11},{10,... | collective-permute-start | bytes 319496 | tf_op jit(solution)/shard_map/ppermute | solution.py:493
  65.5 4.8 %collective-permute-start.9 = (f32[104,256]{1,0:T(8,128)S(1)}, f32[104,256]{1,0:T(8,128)S(1)}, u32[]{:S(2)}, u32[]{:S(2)}) collective-permute-start(f32[104,256]{1,0:T(8,128)S(1)} %add.74), channel_id=1, source_target_pairs={{0,16},{16,0},{1,17},{17,1},{2,18},{18,2},{3,19},{19,3},{4,20},{20... | collective-permute-start | bytes 319496 | tf_op jit(solution)/shard_map/ppermute | solution.py:493
  70.3 4.8 %collective-permute-start.10 = (f32[104,256]{1,0:T(8,128)S(1)}, f32[104,256]{1,0:T(8,128)S(1)}, u32[]{:S(2)}, u32[]{:S(2)}) collective-permute-start(f32[104,256]{1,0:T(8,128)S(1)} %add.75), channel_id=1, source_target_pairs={{0,8},{4,12},{8,0},{12,4},{1,9},{5,13},{9,1},{13,5},{2,10},{6,14},... | collective-permute-start | bytes 319496 | tf_op jit(solution)/shard_map/ppermute | solution.py:502
  75.1 1.5 %collective-permute-start.11 = (f32[208,256]{1,0:T(8,128)S(1)}, f32[208,256]{1,0:T(8,128)S(1)}, u32[]{:S(2)}, u32[]{:S(2)}) collective-permute-start(f32[208,256]{1,0:T(8,128)S(1)} %maximum_select_fusion.mine_ref), channel_id=1, source_target_pairs={{0,4},{4,0},{8,12},{12,8},{1,5},{5,1},{9,13},{13,9},{2,6},{6,2},{1... | collective-permute-start | bytes 638984 | tf_op jit(solution)/shard_map/ppermute | solution.py:570
